TPU v7x, 128 devices: a whole 4x4x4 slice. The times are simulated.
128 devices in a mesh: batch: 1, k: 128 (over z, y, x, core).
Axes of the slice: x: 4, y: 4, z: 4, core: 2. Of those that a mesh axis runs over, the one named last changes fastest.
Arguments:
- a_vals: bfloat16 [128, 4, 128, 128], P(('batch', 'k'))
- b_vals: bfloat16 [128, 4, 128, 128], P(('batch', 'k'))
- pair_list: int32 [128, 4, 256, 2], P(('batch', 'k'))
- plist_idx: int32 [128, 256, 2], P(('batch', 'k'))
- c_idx: int32 [128, 16, 2], P(('batch', 'k'))
Outputs:
- output: float32 [128, 16, 128, 128], P(('batch', 'k'))
All inputs are finite; a program needn't handle non-finite values.
Results may differ from a plain program's by a relative error of at most 0.001.
Values are sent between devices in bfloat16 or wider.
A program may use at most 1 GiB of HBM per device.

v0:
```python
import jax
import jax.numpy as jnp
from jax import lax
from jax.sharding import PartitionSpec as P


def owner_sum(recv_coords, owned_idx, recv_blocks):
    matched = ((recv_coords[None, :, 0] == owned_idx[:, None, 0]) & (recv_coords[None, :, 1] == owned_idx[:, None, 1]) & (recv_coords[None, :, 0] >= 0))
    return jnp.einsum("us,sbd->ubd", matched.astype(jnp.bfloat16), recv_blocks, preferred_element_type=jnp.float32)


def solution(mesh):
    groups = mesh.shape["k"]
    dev_spec = P(("batch", "k"))

    def per_device(a_loc, b_loc, pair_loc, coord_loc, cidx_loc):
        a_blocks = a_loc[0]
        b_blocks = b_loc[0]
        num_cols = pair_loc.shape[2]
        seg_len = num_cols // groups
        blk_size = a_blocks.shape[-1]

        def pair_step(running, pair_rank):
            is_pair = pair_rank[:, 0] >= 0
            left_ops = jnp.take(a_blocks, jnp.maximum(pair_rank[:, 0], 0), axis=0)
            left_ops = jnp.where(is_pair[:, None, None], left_ops, jnp.zeros((), jnp.bfloat16))
            right_ops = jnp.take(b_blocks, jnp.maximum(pair_rank[:, 1], 0), axis=0)
            product = jnp.einsum("sab,sbc->sac", left_ops, right_ops, preferred_element_type=jnp.float32)
            return running + product, None

        start_acc = jnp.zeros((num_cols, blk_size, blk_size), jnp.float32)
        scan_out = lax.scan(pair_step, start_acc, pair_loc[0])
        sent_blocks = scan_out[0].astype(jnp.bfloat16).reshape(groups, seg_len, blk_size, blk_size)
        recv_blocks = lax.all_to_all(sent_blocks, "k", 0, 0, tiled=True)
        recv_coords = lax.all_to_all(coord_loc[0].reshape(groups, seg_len, 2), "k", 0, 0, tiled=True)
        summed = owner_sum(recv_coords.reshape(num_cols, 2), cidx_loc[0], recv_blocks.reshape(num_cols, blk_size, blk_size))
        return summed[None]

    return jax.shard_map(per_device, mesh=mesh, in_specs=(dev_spec, dev_spec, dev_spec, dev_spec, dev_spec), out_specs=dev_spec, check_vma=False)
```

profile of v0, /device:TPU:1, one launch (start us, length us, event | category | flops | bytes accessed | tf_op | source)
XLA Modules:
  0.0 300.9 jit_solution(3183840280719474201)
XLA Ops:
  0.0 0.8 reshape_squeeze.3
  0.8 0.8 copy.14
  1.6 12.0 %all-to-all-start = ((s32[128,2,2]{1,2,0:T(2,128)}), s32[128,2,2]{1,2,0:T(2,128)}, u32[]{:S(2)}, u32[]{:S(2)}) async-start(s32[128,2,2]{1,2,0:T(2,128)} %copy.14), calls=%async_computation | async-start | bytes 262144 | tf_op jit(solution)/shard_map/all_to_all | solution.py:35
  13.6 139.7 %while.11 = (s32[]{:T(128)}, f32[256,128,128]{2,1,0:T(8,128)}, s32[4,256,2]{1,2,0:T(2,128)}, bf16[4,128,128]{2,1,0:T(8,128)(2,1)}, bf16[4,128,128]{2,1,0:T(8,128)(2,1)}, /*index=5*/s32[]{:T(128)}, s32[]{:T(128)}) while((s32[]{:T(128)}, f32[256,128,128]{2,1,0:T(8,128)}, s32[4,256,2]{1,2,0:T(2,128)}, bf16[4,128,128]{2,1,0:T(8,128)(2,1)}, ...), condition=%wide.region_1.0_spmd.clone, body=%wide.region_0.2_spmd.clone.sunk | while | flops 1094720768 | bytes 84439680 | solution.py:32
  13.6 0.7 dynamic-slice_bitcast_fusion.2
  14.3 0.0 copy-start
  14.3 9.3 %gather_fusion = bf16[256,128,128]{2,1,0:T(8,128)(2,1)} fusion(bf16[4,128,128]{2,1,0:T(8,128)(2,1)} %get-tuple-element.127, s32[1024]{0:T(1024)S(1)} %pad_clamp_fusion.4), kind=kCustom, calls=%fused_computation.1.clone.clone.1 | custom fusion | bytes 16778240 | tf_op jit(solution)/shard_map/while/body/eval_jaxpr/jit(_take)/gather | solution.py:27
  23.6 8.3 %gather_fusion.1 = bf16[256,128,128]{2,1,0:T(8,128)(2,1)} fusion(bf16[4,128,128]{2,1,0:T(8,128)(2,1)S(1)} %copy-done, s32[1024]{0:T(1024)S(1)} %pad_clamp_fusion.5), kind=kCustom, calls=%fused_computation.clone.clone.1 | custom fusion | bytes 16778240 | tf_op jit(solution)/shard_map/while/body/eval_jaxpr/jit(_take)/gather | solution.py:25
  32.0 10.9 %select_add_fusion.2 = f32[256,128,128]{2,1,0:T(8,128)} fusion(f32[256,128,128]{2,1,0:T(8,128)} %get-tuple-element.117, bf16[256,128,128]{2,1,0:T(8,128)(2,1)} %gather_fusion, bf16[256,128,128]{2,1,0:T(8,128)(2,1)} %gather_fusion.1, pred[256]{0:T(512)(128)(4,1)S(1)} %get-tuple-element.107, pred[256]{0:T(512)(128)(4,1)S(1)} %get-tuple-element.108, ...), kind=kOutput, calls=%fused_computation.2.clone.1 | convolution fusion | flops 1094713344 | bytes 50332416 | tf_op jit(solution)/shard_map/while/body/eval_jaxpr/sab,sbc->sac/dot_general | solution.py:28
  42.9 0.7 dynamic-slice_bitcast_fusion.2
  43.6 9.2 %gather_fusion = bf16[256,128,128]{2,1,0:T(8,128)(2,1)} fusion(bf16[4,128,128]{2,1,0:T(8,128)(2,1)} %get-tuple-element.127, s32[1024]{0:T(1024)S(1)} %pad_clamp_fusion.4), kind=kCustom, calls=%fused_computation.1.clone.clone.1 | custom fusion | bytes 16778240 | tf_op jit(solution)/shard_map/while/body/eval_jaxpr/jit(_take)/gather | solution.py:27
  52.8 8.2 %gather_fusion.1 = bf16[256,128,128]{2,1,0:T(8,128)(2,1)} fusion(bf16[4,128,128]{2,1,0:T(8,128)(2,1)S(1)} %copy-done, s32[1024]{0:T(1024)S(1)} %pad_clamp_fusion.5), kind=kCustom, calls=%fused_computation.clone.clone.1 | custom fusion | bytes 16778240 | tf_op jit(solution)/shard_map/while/body/eval_jaxpr/jit(_take)/gather | solution.py:25
  61.1 18.6 %select_add_fusion.2 = f32[256,128,128]{2,1,0:T(8,128)} fusion(f32[256,128,128]{2,1,0:T(8,128)} %get-tuple-element.117, bf16[256,128,128]{2,1,0:T(8,128)(2,1)} %gather_fusion, bf16[256,128,128]{2,1,0:T(8,128)(2,1)} %gather_fusion.1, pred[256]{0:T(512)(128)(4,1)S(1)} %get-tuple-element.107, pred[256]{0:T(512)(128)(4,1)S(1)} %get-tuple-element.108, ...), kind=kOutput, calls=%fused_computation.2.clone.1 | convolution fusion | flops 1094713344 | bytes 50332416 | tf_op jit(solution)/shard_map/while/body/eval_jaxpr/sab,sbc->sac/dot_general | solution.py:28
  79.7 0.7 dynamic-slice_bitcast_fusion.2
  80.4 0.0 copy-start
  80.4 9.2 %gather_fusion = bf16[256,128,128]{2,1,0:T(8,128)(2,1)} fusion(bf16[4,128,128]{2,1,0:T(8,128)(2,1)} %get-tuple-element.127, s32[1024]{0:T(1024)S(1)} %pad_clamp_fusion.4), kind=kCustom, calls=%fused_computation.1.clone.clone.1 | custom fusion | bytes 16778240 | tf_op jit(solution)/shard_map/while/body/eval_jaxpr/jit(_take)/gather | solution.py:27
  89.6 8.2 %gather_fusion.1 = bf16[256,128,128]{2,1,0:T(8,128)(2,1)} fusion(bf16[4,128,128]{2,1,0:T(8,128)(2,1)S(1)} %copy-done, s32[1024]{0:T(1024)S(1)} %pad_clamp_fusion.5), kind=kCustom, calls=%fused_computation.clone.clone.1 | custom fusion | bytes 16778240 | tf_op jit(solution)/shard_map/while/body/eval_jaxpr/jit(_take)/gather | solution.py:25
  97.8 18.6 %select_add_fusion.2 = f32[256,128,128]{2,1,0:T(8,128)} fusion(f32[256,128,128]{2,1,0:T(8,128)} %get-tuple-element.117, bf16[256,128,128]{2,1,0:T(8,128)(2,1)} %gather_fusion, bf16[256,128,128]{2,1,0:T(8,128)(2,1)} %gather_fusion.1, pred[256]{0:T(512)(128)(4,1)S(1)} %get-tuple-element.107, pred[256]{0:T(512)(128)(4,1)S(1)} %get-tuple-element.108, ...), kind=kOutput, calls=%fused_computation.2.clone.1 | convolution fusion | flops 1094713344 | bytes 50332416 | tf_op jit(solution)/shard_map/while/body/eval_jaxpr/sab,sbc->sac/dot_general | solution.py:28
  116.5 0.7 dynamic-slice_bitcast_fusion.2
  117.2 0.0 copy-start
  117.2 9.2 %gather_fusion = bf16[256,128,128]{2,1,0:T(8,128)(2,1)} fusion(bf16[4,128,128]{2,1,0:T(8,128)(2,1)} %get-tuple-element.127, s32[1024]{0:T(1024)S(1)} %pad_clamp_fusion.4), kind=kCustom, calls=%fused_computation.1.clone.clone.1 | custom fusion | bytes 16778240 | tf_op jit(solution)/shard_map/while/body/eval_jaxpr/jit(_take)/gather | solution.py:27
  126.4 8.2 %gather_fusion.1 = bf16[256,128,128]{2,1,0:T(8,128)(2,1)} fusion(bf16[4,128,128]{2,1,0:T(8,128)(2,1)S(1)} %copy-done, s32[1024]{0:T(1024)S(1)} %pad_clamp_fusion.5), kind=kCustom, calls=%fused_computation.clone.clone.1 | custom fusion | bytes 16778240 | tf_op jit(solution)/shard_map/while/body/eval_jaxpr/jit(_take)/gather | solution.py:25
  134.6 18.6 %select_add_fusion.2 = f32[256,128,128]{2,1,0:T(8,128)} fusion(f32[256,128,128]{2,1,0:T(8,128)} %get-tuple-element.117, bf16[256,128,128]{2,1,0:T(8,128)(2,1)} %gather_fusion, bf16[256,128,128]{2,1,0:T(8,128)(2,1)} %gather_fusion.1, pred[256]{0:T(512)(128)(4,1)S(1)} %get-tuple-element.107, pred[256]{0:T(512)(128)(4,1)S(1)} %get-tuple-element.108, ...), kind=kOutput, calls=%fused_computation.2.clone.1 | convolution fusion | flops 1094713344 | bytes 50332416 | tf_op jit(solution)/shard_map/while/body/eval_jaxpr/sab,sbc->sac/dot_general | solution.py:28
  153.2 6.6 %convert_element_type.4 = bf16[256,128,128]{2,1,0:T(8,128)(2,1)S(1)} convert(f32[256,128,128]{2,1,0:T(8,128)} %get-tuple-element.33) | non-fusion elementwise | flops 4194304 | bytes 25165824 | tf_op jit(solution)/shard_map/convert_element_type | solution.py:33
  159.9 8.0 %copy.16 = bf16[128,2,128,128]{3,1,2,0:T(2,128)(2,1)} copy(bf16[128,2,128,128]{3,2,1,0:T(8,128)(2,1)S(1)} %bitcast.34) | data formatting | bytes 16777216 | tf_op jit(solution)/shard_map/reshape | solution.py:33
  167.9 10.3 %all-to-all-start.1 = ((bf16[128,2,128,128]{3,1,2,0:T(2,128)(2,1)}), bf16[128,2,128,128]{3,1,2,0:T(2,128)(2,1)}, u32[]{:S(2)}, u32[]{:S(2)}) async-start(bf16[128,2,128,128]{3,1,2,0:T(2,128)(2,1)} %copy.16), calls=%async_computation.1 | async-start | bytes 16777216 | tf_op jit(solution)/shard_map/all_to_all | solution.py:34
  178.2 0.9 copy.15
  179.1 0.1 reshape.34
  179.3 111.8 %all-to-all-done.1 = bf16[128,2,128,128]{3,1,2,0:T(2,128)(2,1)} async-done(((bf16[128,2,128,128]{3,1,2,0:T(2,128)(2,1)}), bf16[128,2,128,128]{3,1,2,0:T(2,128)(2,1)}, u32[]{:S(2)}, u32[]{:S(2)}) %all-to-all-start.1) | async-done | bytes 8388640 | tf_op jit(solution)/shard_map/all_to_all | solution.py:34
  291.1 7.3 %copy.17 = bf16[128,2,128,128]{3,1,0,2:T(2,128)(2,1)S(1)} copy(bf16[128,2,128,128]{3,1,2,0:T(2,128)(2,1)} %all-to-all-done.1) | data formatting | bytes 16777216 | tf_op jit(solution)/shard_map/all_to_all | solution.py:34
  298.4 1.2 convolution_bitcast_fusion
  299.6 1.3 copy.18
  (40 shorter events, 0.3 us)
Async XLA Ops:
  1.6 166.4 %all-to-all-start = ((s32[128,2,2]{1,2,0:T(2,128)}), s32[128,2,2]{1,2,0:T(2,128)}, u32[]{:S(2)}, u32[]{:S(2)}) async-start(s32[128,2,2]{1,2,0:T(2,128)} %copy.14), calls=%async_computation | async-start | bytes 262144 | tf_op jit(solution)/shard_map/all_to_all | solution.py:35
  14.3 9.3 %copy-start = (bf16[4,128,128]{2,1,0:T(8,128)(2,1)S(1)}, bf16[4,128,128]{2,1,0:T(8,128)(2,1)}, u32[]{:S(2)}) copy-start(bf16[4,128,128]{2,1,0:T(8,128)(2,1)} %get-tuple-element.126) | copy-start | bytes 393220 | tf_op jit(solution)/shard_map/while
  43.6 9.2 %copy-start = (bf16[4,128,128]{2,1,0:T(8,128)(2,1)S(1)}, bf16[4,128,128]{2,1,0:T(8,128)(2,1)}, u32[]{:S(2)}) copy-start(bf16[4,128,128]{2,1,0:T(8,128)(2,1)} %get-tuple-element.126) | copy-start | bytes 393220 | tf_op jit(solution)/shard_map/while
  80.4 9.2 %copy-start = (bf16[4,128,128]{2,1,0:T(8,128)(2,1)S(1)}, bf16[4,128,128]{2,1,0:T(8,128)(2,1)}, u32[]{:S(2)}) copy-start(bf16[4,128,128]{2,1,0:T(8,128)(2,1)} %get-tuple-element.126) | copy-start | bytes 393220 | tf_op jit(solution)/shard_map/while
  117.2 9.2 %copy-start = (bf16[4,128,128]{2,1,0:T(8,128)(2,1)S(1)}, bf16[4,128,128]{2,1,0:T(8,128)(2,1)}, u32[]{:S(2)}) copy-start(bf16[4,128,128]{2,1,0:T(8,128)(2,1)} %get-tuple-element.126) | copy-start | bytes 393220 | tf_op jit(solution)/shard_map/while
  167.9 10.3 %copy-start.1 = (s32[1,16,2]{1,2,0:T(2,128)S(1)}, s32[1,16,2]{1,2,0:T(2,128)}, u32[]{:S(2)}) copy-start(s32[1,16,2]{1,2,0:T(2,128)} %param.13) | copy-start | bytes 388
  167.9 123.1 %all-to-all-start.1 = ((bf16[128,2,128,128]{3,1,2,0:T(2,128)(2,1)}), bf16[128,2,128,128]{3,1,2,0:T(2,128)(2,1)}, u32[]{:S(2)}, u32[]{:S(2)}) async-start(bf16[128,2,128,128]{3,1,2,0:T(2,128)(2,1)} %copy.16), calls=%async_computation.1 | async-start | bytes 16777216 | tf_op jit(solution)/shard_map/all_to_all | solution.py:34
where the time goes:
time: 304 us; the launch traced here: 301 us
  waiting for transfers between devices  112 us (37%)
  local copies, waits for them, and re-layouts  91.8 us (30%)
  matrix products  68.1 us (22%)
  starting transfers between devices  22.2 us (7%)
  other arithmetic  6.91 us (2%)
    all_to_all x1, waiting for transfers between devices, per_device(): recv_blocks = lax.all_to_all(sent_blocks, 'k', 0, 0, tiled=True)  112 us
    dot_general x4, matrix products, pair_step(): jnp.einsum('sab,sbc->sac', left_ops, right_ops, preferred_element_type=jn...  66.8 us
    gather x4, local copies, waits for them, and re-layouts, pair_step(): right_ops = jnp.take(b_blocks, jnp.maximum(pair_rank[:, 1], 0), axis=0)  36.8 us
    gather x4, local copies, waits for them, and re-layouts, pair_step(): left_ops = jnp.take(a_blocks, jnp.maximum(pair_rank[:, 0], 0), axis=0)  33 us
    all_to_all x1, starting transfers between devices, per_device(): lax.all_to_all(coord_loc[0].reshape(groups, seg_len, 2), 'k', 0, 0, tiled...  12 us
    all_to_all x1, starting transfers between devices, per_device(): recv_blocks = lax.all_to_all(sent_blocks, 'k', 0, 0, tiled=True)  10.3 us
    reshape x1, local copies, waits for them, and re-layouts, per_device(): scan_out[0].astype(jnp.bfloat16)  8.05 us
    all_to_all x1, local copies, waits for them, and re-layouts, per_device(): recv_blocks = lax.all_to_all(sent_blocks, 'k', 0, 0, tiled=True)  7.3 us
  transfers between devices with their start and end apart: 2, of which 1 were waited for; matrix products, arithmetic and copies ran while one was open for 52% of the time, Pallas kernels for 0%

commit v1 on v0

v1 whole, which is shorter than its diff:
```python
import functools

import jax
import jax.numpy as jnp
from jax import lax
from jax.experimental import pallas as pl
from jax.experimental.pallas import tpu as pltpu
from jax.sharding import PartitionSpec as P

RING = 4
SIDE = 4
PLANE = 32
LINES = PLANE // 2
SLOTS = 8
NOPAIR = 16
NOSLOT = PLANE * SLOTS


def order_of(j):
    return j + (j // 2) * (1 - 2 * (j % 2))


def kernel(a_ref, b_ref, tbl_ref, crow_ref, out_ref, held, prod0, prod1, parts, acc, opp, fin, tblb, cb, selv,
           tbl_s, sel_s, local_sem, own_sem, sib_sem, f_sem, s_sem, d_sem, tsend_sem, trecv_sem, csend_sem, crecv_sem,
           tloc_sem, smem_sem, sel_sem, rs_send, opp_sem, fin_sem):
    me = lax.axis_index("k")
    z = me // PLANE
    d = me % PLANE
    y = d // 8
    x = (d // 2) % 4
    c = d % 2
    n_own = out_ref.shape[0]
    half_own = n_own // 2

    def dev(zz, yy, xx, cc):
        return {"k": ((zz * 4 + yy) * 4 + xx) * 2 + cc}

    sibling = dev(z, y, x, 1 - c)

    def f_dev(off):
        return dev(z, (y + off * c) % 4, (x + off * (1 - c)) % 4, c)

    def s_dev(off):
        return dev(z, (y + off * (1 - c)) % 4, (x + off * c) % 4, c)

    def z_dev(off):
        return {"k": ((z + off) % 4) * PLANE + d}

    def slot_of(core, df, ds):
        sx = (x + df * (1 - core) + ds * core) % 4
        sy = (y + df * core + ds * (1 - core)) % 4
        return sy * 4 + sx

    barrier = pltpu.get_barrier_semaphore()

    def greet(r, carry):
        pl.semaphore_signal(barrier, inc=1, device_id={"k": z * PLANE + (d + r) % PLANE},
                            device_id_type=pl.DeviceIdType.MESH)
        return carry

    lax.fori_loop(1, PLANE, greet, 0)
    for off in (1, 2, 3):
        pl.semaphore_signal(barrier, inc=1, device_id=z_dev(off), device_id_type=pl.DeviceIdType.MESH)

    my_slot = y * 4 + x

    def half(core, slot, h):
        return held.at[core, slot, pl.ds(4 * h, 4)]

    loads = [
        pltpu.make_async_copy(ref.at[pl.ds(2 * h, 2)], held.at[c, my_slot, pl.ds(4 * h + 2 * w, 2)],
                              local_sem.at[2 * h + w])
        for h in (0, 1) for w, ref in enumerate((a_ref, b_ref))
    ]
    for cp in loads:
        cp.start()
    tloc = pltpu.make_async_copy(tbl_ref.at[pl.ds(2 * d, 2)], tblb.at[pl.ds(2 * d, 2)], tloc_sem.at[0])
    cloc = pltpu.make_async_copy(crow_ref, cb.at[pl.ds(z, 1)], tloc_sem.at[1])
    tloc.start()
    cloc.start()

    zero = jnp.zeros(prod0.shape[1:], jnp.float32)
    prod0[NOPAIR] = zero
    prod1[NOPAIR] = zero
    parts[NOSLOT] = zero

    pl.semaphore_wait(barrier, PLANE - 1 + 3)

    def push(core, slot, h, target, send_sem, recv):
        pltpu.make_async_remote_copy(
            src_ref=half(core, slot, h), dst_ref=half(core, slot, h), send_sem=send_sem,
            recv_sem=recv.at[slot, h], device_id=target, device_id_type=pl.DeviceIdType.MESH).start()

    def arrived(core, slot, h, recv):
        pltpu.make_async_copy(half(core, slot, h), half(core, slot, h), recv.at[slot, h]).wait()

    def to_sibling(slot, h):
        push(c, slot, h, sibling, d_sem.at[0], sib_sem)

    for cp in loads:
        cp.wait()
    for h in (0, 1):
        for off in (1, 3):
            push(c, my_slot, h, f_dev(off), f_sem.at[0], own_sem)
            push(c, my_slot, h, s_dev(off), s_sem.at[0], own_sem)
        to_sibling(my_slot, h)

    def send_tables(r, carry):
        peer = (d + r) % PLANE
        pltpu.make_async_remote_copy(
            src_ref=tbl_ref.at[pl.ds(2 * peer, 2)], dst_ref=tblb.at[pl.ds(2 * d, 2)], send_sem=tsend_sem.at[0],
            recv_sem=trecv_sem.at[0], device_id={"k": z * PLANE + peer},
            device_id_type=pl.DeviceIdType.MESH).start()
        return carry

    lax.fori_loop(1, PLANE, send_tables, 0)
    for off in (1, 2, 3):
        pltpu.make_async_remote_copy(
            src_ref=crow_ref, dst_ref=cb.at[pl.ds(z, 1)], send_sem=csend_sem.at[0], recv_sem=crecv_sem.at[0],
            device_id=z_dev(off), device_id_type=pl.DeviceIdType.MESH).start()

    def bytes_wait(ref, sem):
        pltpu.make_async_copy(ref, ref, sem).wait()

    tloc.wait()
    cloc.wait()
    bytes_wait(tblb.at[pl.ds(0, 2 * (PLANE - 1))], trecv_sem.at[0])
    bytes_wait(cb.at[pl.ds(0, 3)], crecv_sem.at[0])
    to_smem = pltpu.make_async_copy(tblb, tbl_s, smem_sem.at[0])
    to_smem.start()
    codes = jnp.concatenate([tblb[pl.ds(2 * p + 1, 1), 0] for p in range(PLANE)], axis=0)
    wanted = jnp.sum(cb[...], axis=0)
    row = lax.broadcasted_iota(jnp.int32, codes.shape, 0)
    lane = lax.broadcasted_iota(jnp.int32, codes.shape, 1)
    index = row * SLOTS + 2 * ((lane % 64) // n_own) + lane // 64
    hit = jnp.where(codes == wanted, index - NOSLOT, 0)
    selv[...] = NOSLOT + jnp.where(hit != 0, hit, pltpu.roll(hit, 64, 1))
    to_smem.wait()

    def compute(core, slot, prod):
        lhs = jnp.concatenate([held[core, slot, i] for i in (0, 1, 4, 5)], axis=0)
        rows = lhs.shape[0] // 4
        cols = held.shape[-1]
        for pair in (0, 1):
            rhs = jnp.concatenate([held[core, slot, 2 + 4 * pair], held[core, slot, 3 + 4 * pair]], axis=1)
            res = jnp.dot(lhs, rhs, preferred_element_type=jnp.float32)
            for a in range(4):
                for b in (0, 1):
                    prod[a * 4 + 2 * pair + b] = res[a * rows:(a + 1) * rows, b * cols:(b + 1) * cols]
        src = slot * 2 + core
        for j in range(SLOTS):
            total = prod[tbl_s[2 * src, 0, 4 * j]]
            for u in (1, 2, 3):
                total = total + prod[tbl_s[2 * src, 0, 4 * j + u]]
            parts[src * SLOTS + j] = total.astype(jnp.bfloat16).astype(jnp.float32)

    def both(df, ds):
        slot = slot_of(1 - c, df, ds)
        for h in (0, 1):
            arrived(1 - c, slot, h, sib_sem)
        compute(c, slot_of(c, df, ds), prod0)
        compute(1 - c, slot, prod1)

    both(0, 0)
    to_sel = pltpu.make_async_copy(selv, sel_s, sel_sem.at[0])
    to_sel.start()

    def first_line(j, carry):
        df = order_of(j)
        slot = slot_of(c, df, 0)
        for h in (0, 1):
            arrived(c, slot, h, own_sem)
            if h == 0:
                @pl.when(df == 3)
                def _():
                    push(c, slot, 0, f_dev(1), f_sem.at[0], own_sem)
            else:
                @pl.when(df == 1)
                def _():
                    push(c, slot, 1, f_dev(3), f_sem.at[0], own_sem)
            for off in (1, 3):
                push(c, slot, h, s_dev(off), s_sem.at[0], own_sem)
            to_sibling(slot, h)
        both(df, 0)
        return carry

    lax.fori_loop(1, 4, first_line, 0)

    def neighbours(k, carry):
        df = order_of(k // 2)
        ds = 1 + 2 * (k % 2)
        slot = slot_of(c, df, ds)
        for h in (0, 1):
            arrived(c, slot, h, own_sem)
            if h == 0:
                @pl.when(ds == 3)
                def _():
                    push(c, slot, 0, s_dev(1), s_sem.at[0], own_sem)
            else:
                @pl.when(ds == 1)
                def _():
                    push(c, slot, 1, s_dev(3), s_sem.at[0], own_sem)
            to_sibling(slot, h)
        both(df, ds)
        return carry

    lax.fori_loop(0, 8, neighbours, 0)

    def opposite(j, carry):
        df = order_of(j)
        slot = slot_of(c, df, 2)
        for h in (0, 1):
            arrived(c, slot, h, own_sem)
            to_sibling(slot, h)
        both(df, 2)
        return carry

    lax.fori_loop(0, 4, opposite, 0)
    to_sel.wait()

    def block_sum(zz, t):
        def add(p4, total):
            for u in range(8):
                total = total + parts[sel_s[p4 * 8 + u, zz * n_own + t]]
            return total
        return lax.fori_loop(0, PLANE // 8, add, zero)

    def z_push(rel, t, dst, recv, off):
        zz = (z + rel) % 4
        pltpu.make_async_remote_copy(
            src_ref=acc.at[zz, t], dst_ref=dst, send_sem=rs_send.at[0], recv_sem=recv, device_id=z_dev(off),
            device_id_type=pl.DeviceIdType.MESH).start()

    z_up, z_two, z_down = (z + 1) % 4, (z + 2) % 4, (z + 3) % 4

    def far(t, carry):
        acc[z_two, t] = block_sum(z_two, t)
        acc[z_two, t + half_own] = block_sum(z_two, t + half_own)
        z_push(2, t, opp.at[0, t], opp_sem.at[0, t], 1)
        z_push(2, t + half_own, opp.at[1, t], opp_sem.at[1, t], 3)
        return carry

    lax.fori_loop(0, half_own, far, 0)

    def near(t, carry):
        acc[z_up, t + half_own] = block_sum(z_up, t + half_own)
        acc[z_down, t] = block_sum(z_down, t)
        z_push(1, t + half_own, fin.at[0, t + half_own], fin_sem.at[0, t + half_own], 1)
        z_push(3, t, fin.at[1, t], fin_sem.at[1, t], 3)
        return carry

    lax.fori_loop(0, half_own, near, 0)

    def combined(t, carry):
        up = block_sum(z_up, t)
        down = block_sum(z_down, t + half_own)
        bytes_wait(opp.at[0, t], opp_sem.at[0, t])
        bytes_wait(opp.at[1, t], opp_sem.at[1, t])
        acc[z_up, t] = up + opp[0, t]
        acc[z_down, t + half_own] = down + opp[1, t]
        z_push(1, t, fin.at[0, t], fin_sem.at[0, t], 1)
        z_push(3, t + half_own, fin.at[1, t + half_own], fin_sem.at[1, t + half_own], 3)
        return carry

    lax.fori_loop(0, half_own, combined, 0)

    def mine(t, carry):
        acc[z, t] = block_sum(z, t)
        return carry

    lax.fori_loop(0, n_own, mine, 0)

    def finish(t, carry):
        for tt in (t, t + half_own):
            bytes_wait(fin.at[0, tt], fin_sem.at[0, tt])
            bytes_wait(fin.at[1, tt], fin_sem.at[1, tt])
            out_ref[tt] = acc[z, tt] + (fin[0, tt] + fin[1, tt])
        return carry

    lax.fori_loop(0, half_own, finish, 0)

    bytes_wait(held.at[0, pl.ds(0, 3)], f_sem.at[0])
    bytes_wait(held.at[0, pl.ds(0, 12)], s_sem.at[0])
    bytes_wait(held.at[0], d_sem.at[0])
    bytes_wait(tblb.at[pl.ds(0, 2 * (PLANE - 1))], tsend_sem.at[0])
    bytes_wait(cb.at[pl.ds(0, 3)], csend_sem.at[0])
    bytes_wait(acc.at[pl.ds(0, 3)], rs_send.at[0])


def tables(pairs, coords, cidx, z):
    n_own = cidx.shape[0]
    pid = jnp.where(pairs[..., 0] >= 0, pairs[..., 0] * 4 + pairs[..., 1], NOPAIR)
    pid = pid.reshape(4, RING, PLANE, 2).transpose(2, 1, 3, 0).reshape(PLANE, 1, 4 * SLOTS)
    pid = jnp.pad(pid, ((0, 0), (0, 0), (0, 128 - 4 * SLOTS)))
    code = jnp.where(coords[:, 0] >= 0, coords[:, 0] * 256 + coords[:, 1], -1)
    code = code.reshape(RING, PLANE, 2).transpose(1, 2, 0)
    code = jnp.broadcast_to(code[..., None], (PLANE, 2, RING, n_own)).reshape(PLANE, 1, 128)
    tbl = jnp.concatenate([pid, code], axis=1).reshape(2 * PLANE, 1, 128)
    own = cidx[:, 0] * 256 + cidx[:, 1]
    at = jnp.arange(RING)[:, None] == z
    crow = jnp.broadcast_to(jnp.where(at, own[None, :], 0)[None], (2, RING, n_own)).reshape(1, 1, 128)
    return tbl, crow


def solution(mesh):
    dev_spec = P(("batch", "k"))

    def per_device(a_loc, b_loc, pair_loc, coord_loc, cidx_loc):
        a, b, cidx = a_loc[0], b_loc[0], cidx_loc[0]
        n_own = cidx.shape[0]
        rows, cols = a.shape[1], b.shape[2]
        tbl, crow = tables(pair_loc[0], coord_loc[0], cidx, lax.axis_index("k") // PLANE)
        blk = (rows, cols)
        f32, i32 = jnp.float32, jnp.int32
        dma = pltpu.SemaphoreType.DMA
        out = pl.pallas_call(
            kernel,
            out_shape=jax.ShapeDtypeStruct((n_own,) + blk, f32),
            in_specs=[pl.BlockSpec(memory_space=pl.ANY)] * 4,
            out_specs=pl.BlockSpec(memory_space=pltpu.VMEM),
            scratch_shapes=[
                pltpu.VMEM((2, LINES, 8) + blk, jnp.bfloat16),
                pltpu.VMEM((NOPAIR + 1,) + blk, f32),
                pltpu.VMEM((NOPAIR + 1,) + blk, f32),
                pltpu.VMEM((NOSLOT + 1,) + blk, f32),
                pltpu.VMEM((RING, n_own) + blk, f32),
                pltpu.VMEM((2, n_own // 2) + blk, f32),
                pltpu.VMEM((2, n_own) + blk, f32),
                pltpu.VMEM((2 * PLANE, 1, 128), i32),
                pltpu.VMEM((RING, 1, 128), i32),
                pltpu.VMEM((PLANE, 128), i32),
                pltpu.SMEM((2 * PLANE, 1, 128), i32),
                pltpu.SMEM((PLANE, 128), i32),
                dma((4,)), dma((LINES, 2)), dma((LINES, 2)), dma((1,)), dma((1,)), dma((1,)), dma((1,)), dma((1,)),
                dma((1,)), dma((1,)), dma((2,)), dma((1,)), dma((1,)), dma((1,)), dma((2, n_own // 2)),
                dma((2, n_own)),
            ],
            compiler_params=pltpu.CompilerParams(collective_id=0, has_side_effects=True,
                                                 vmem_limit_bytes=60 * 1024 * 1024),
        )(a, b, tbl, crow)
        return out[None]

    return jax.shard_map(per_device, mesh=mesh, in_specs=(dev_spec,) * 5, out_specs=dev_spec, check_vma=False)
```

time: 304 us -> 97.9 us (0.32)
  waiting for transfers between devices: 112 us -> 0 us
  Pallas kernels: 0 us -> 92.2 us
  local copies, waits for them, and re-layouts: 91.8 us -> 5.35 us
  matrix products: 68.1 us -> 0 us
  starting transfers between devices: 22.2 us -> 0 us
  other arithmetic: 6.91 us -> 0.14 us
    all_to_all x2 -> x0, waiting for transfers between devices: 112 us -> none  [the longest x1 112 us: per_device(): recv_blocks = lax.all_to_all(sent_blocks, 'k', 0, 0, tiled=True)]
    pallas_call x0 -> x1, Pallas kernels: none -> 92.2 us  [per_device(): pl.pallas_call(kernel, out_shape=jax.ShapeDtypeStruct((n_own,) + blk, f32...]
    gather x8 -> x0, local copies, waits for them, and re-layouts: 69.7 us -> none  [the longest x4 36.8 us: pair_step(): right_ops = jnp.take(b_blocks, jnp.maximum(pair_rank[:, 1], 0), axis=0)]
    dot_general x5 -> x0, matrix products: 68.1 us -> none  [the longest x4 66.8 us: pair_step(): jnp.einsum('sab,sbc->sac', left_ops, right_ops, preferred_element_type=jn...]
    all_to_all x2 -> x0, starting transfers between devices: 22.2 us -> none  [the longest x1 12 us: per_device(): lax.all_to_all(coord_loc[0].reshape(groups, seg_len, 2), 'k', 0, 0, tiled...]
    all_to_all x2 -> x0, local copies, waits for them, and re-layouts: 8.21 us -> none  [the longest x1 7.3 us: per_device(): recv_blocks = lax.all_to_all(sent_blocks, 'k', 0, 0, tiled=True)]
    reshape x2 -> x1, local copies, waits for them, and re-layouts: 8.18 us -> 0.6 us  [tables(): jnp.broadcast_to(jnp.where(at, own[None, :], 0)[None], (2, RING, n_own))]
    convert_element_type x1 -> x0, other arithmetic: 6.65 us -> none  [per_device(): scan_out[0].astype(jnp.bfloat16)]
  transfers between devices with their start and end apart: 2 -> 0, of which waited for: 1 -> 0; matrix products, arithmetic and copies ran while one was open for 52% -> 0% of each run, Pallas kernels for 0% -> 0%
where the time goes in v1:
time: 97.9 us; the launch traced here: 97.7 us
  Pallas kernels  92.2 us (94%)
  local copies, waits for them, and re-layouts  5.35 us (5%)
    pallas_call x1, Pallas kernels, per_device(): pl.pallas_call(kernel, out_shape=jax.ShapeDtypeStruct((n_own,) + blk, f32...  92.2 us
    unnamed x7, local copies, waits for them, and re-layouts  3.57 us

profile of v1, /device:TPU:1, one launch (start us, length us, event | category | flops | bytes accessed | tf_op | source)
XLA Modules:
  0.0 97.7 jit_solution(6236270217128283241)
XLA Ops:
  0.0 0.0 copy-start.2
  0.0 0.7 copy-done.2
  0.7 0.0 copy-start.1
  0.7 0.0 copy-start
  0.7 0.1 broadcast_select_fusion
  0.8 0.6 copy-done.1
  1.4 0.6 reshape.81.crow_ref
  2.0 0.0 copy-done
  2.0 0.1 select_n.32
  2.1 0.1 copy.20
  2.3 0.1 copy.18
  2.4 0.1 copy.19
  2.5 0.7 copy.21
  3.2 92.2 %shard_map.55 = f32[16,128,128]{2,1,0:T(8,128)} custom-call(bf16[4,128,128]{2,1,0:T(8,128)(2,1)} %bitcast.19, bf16[4,128,128]{2,1,0:T(8,128)(2,1)} %bitcast.20, s32[64,1,128]{2,1,0:T(1,128)} %bitcast.21, s32[1,1,128]{2,1,0:T(1,128)} %reshape.81.crow_ref), custom_call_target="tpu_custom_call" | custom-call | tf_op jit(solution)/shard_map/pallas_call | solution.py:316
  95.5 2.3 %copy.23 = f32[1,16,128,128]{3,2,1,0:T(8,128)} copy(f32[1,16,128,128]{3,2,1,0:T(8,128)} %bitcast.15) | data formatting | bytes 2097152
  (7 shorter events, 0.1 us)
Async XLA Ops:
  0.0 0.7 copy-start.2
  0.7 0.7 copy-start.1
  0.7 1.3 %copy-start = (s32[1,4,256,2]{2,3,1,0:T(2,128)S(1)}, s32[1,4,256,2]{2,3,1,0:T(2,128)}, u32[]{:S(2)}) copy-start(s32[1,4,256,2]{2,3,1,0:T(2,128)} %param.7) | copy-start | bytes 24580

commit v2 on v0

v2 whole, which is shorter than its diff:
```python
import jax
import jax.numpy as jnp
from jax import lax
from jax.experimental import pallas as pl
from jax.experimental.pallas import tpu as pltpu
from jax.sharding import PartitionSpec as P

RING = 4
PLANE = 32
LINES = PLANE // 2
SLOTS = 8
NOPAIR = 16
NOSLOT = PLANE * SLOTS
CHUNKS = 2
GROUP = 2
MESH = pl.DeviceIdType.MESH


def order_of(j):
    return j + (j // 2) * (1 - 2 * (j % 2))


def kernel(a_ref, b_ref, tbl_ref, crow_ref, out_ref, held_b, held_a, prods, parts, acc, opp, fin, tblb, cb, selv,
           tbl_s, sel_s, local_sem, own_sem, sib_sem, f_sem, s_sem, d_sem, tsend_sem, trecv_sem, csend_sem, crecv_sem,
           tloc_sem, smem_sem, sel_sem, rs_send, opp_sem, fin_sem):
    me = lax.axis_index("k")
    z = me // PLANE
    d = me % PLANE
    y = d // 8
    x = (d // 2) % 4
    c = d % 2
    n_own = out_ref.shape[0]
    half_own = n_own // 2
    n_grp = half_own // GROUP
    chunk_rows = out_ref.shape[1] // CHUNKS
    cols = out_ref.shape[2]

    def dev(zz, yy, xx, cc):
        return {"k": ((zz * 4 + yy) * 4 + xx) * 2 + cc}

    sibling = dev(z, y, x, 1 - c)

    def f_dev(off):
        return dev(z, (y + off * c) % 4, (x + off * (1 - c)) % 4, c)

    def s_dev(off):
        return dev(z, (y + off * (1 - c)) % 4, (x + off * c) % 4, c)

    def z_dev(off):
        return {"k": ((z + off) % 4) * PLANE + d}

    def slot_of(core, df, ds):
        sx = (x + df * (1 - core) + ds * core) % 4
        sy = (y + df * core + ds * (1 - core)) % 4
        return sy * 4 + sx

    barrier = pltpu.get_barrier_semaphore()

    def greet(r, carry):
        pl.semaphore_signal(barrier, inc=1, device_id={"k": z * PLANE + (d + r) % PLANE}, device_id_type=MESH)
        return carry

    lax.fori_loop(1, PLANE, greet, 0)
    for off in (1, 2, 3):
        pl.semaphore_signal(barrier, inc=1, device_id=z_dev(off), device_id_type=MESH)

    my_slot = y * 4 + x
    pieces = [held_b] + list(held_a)

    loads = [pltpu.make_async_copy(b_ref, held_b.at[c, my_slot], local_sem.at[0])]
    for ch in range(CHUNKS):
        loads.append(pltpu.make_async_copy(a_ref.at[:, pl.ds(ch * chunk_rows, chunk_rows)], held_a[ch].at[c, my_slot],
                                           local_sem.at[1 + ch]))
    for cp in loads:
        cp.start()
    tloc = pltpu.make_async_copy(tbl_ref.at[pl.ds(2 * d, 2)], tblb.at[pl.ds(2 * d, 2)], tloc_sem.at[0])
    cloc = pltpu.make_async_copy(crow_ref, cb.at[pl.ds(z, 1)], tloc_sem.at[1])
    tloc.start()
    cloc.start()

    zero = jnp.zeros((chunk_rows, cols), jnp.float32)
    for ref in prods:
        ref[NOPAIR] = zero
    for ref in parts:
        ref[NOSLOT] = zero

    pl.semaphore_wait(barrier, PLANE - 1 + 3)

    def whole(k, core, slot):
        return pieces[k].at[core, slot]

    def half(k, core, slot, h):
        return pieces[k].at[core, slot, pl.ds(2 * h, 2)]

    def send(ref, target, send_sem, recv_sem):
        pltpu.make_async_remote_copy(src_ref=ref, dst_ref=ref, send_sem=send_sem, recv_sem=recv_sem,
                                     device_id=target, device_id_type=MESH).start()

    def bytes_wait(ref, sem):
        pltpu.make_async_copy(ref, ref, sem).wait()

    def to_sibling(k, slot):
        send(whole(k, c, slot), sibling, d_sem.at[k], sib_sem.at[k, slot])

    def to_f(k, slot):
        for off in (1, 3):
            send(whole(k, c, slot), f_dev(off), f_sem.at[k], own_sem.at[k, slot, 0])

    def to_s(k, slot):
        for off in (1, 3):
            send(whole(k, c, slot), s_dev(off), s_sem.at[k], own_sem.at[k, slot, 0])

    def got_whole(k, slot):
        bytes_wait(whole(k, c, slot), own_sem.at[k, slot, 0])

    def got_halves(k, slot):
        for h in (0, 1):
            bytes_wait(half(k, c, slot, h), own_sem.at[k, slot, h])

    def line_near(k):
        for df, h, off in ((1, 1, 3), (3, 0, 1)):
            slot = slot_of(c, df, 0)
            got_whole(k, slot)
            send(half(k, c, slot, h), f_dev(off), f_sem.at[k], own_sem.at[k, slot, h])
            to_s(k, slot)
            to_sibling(k, slot)

    def line_far(k):
        slot = slot_of(c, 2, 0)
        got_halves(k, slot)
        to_s(k, slot)
        to_sibling(k, slot)

    def side_near(k, df):
        for ds, h, off in ((1, 1, 3), (3, 0, 1)):
            slot = slot_of(c, df, ds)
            got_whole(k, slot)
            send(half(k, c, slot, h), s_dev(off), s_sem.at[k], own_sem.at[k, slot, h])
            to_sibling(k, slot)

    def side_far(k, df):
        slot = slot_of(c, df, 2)
        got_halves(k, slot)
        to_sibling(k, slot)

    for k in range(1 + CHUNKS):
        loads[k].wait()
        to_f(k, my_slot)
        if k < 2:
            to_s(k, my_slot)
            to_sibling(k, my_slot)

    def send_tables(r, carry):
        peer = (d + r) % PLANE
        pltpu.make_async_remote_copy(
            src_ref=tbl_ref.at[pl.ds(2 * peer, 2)], dst_ref=tblb.at[pl.ds(2 * d, 2)], send_sem=tsend_sem.at[0],
            recv_sem=trecv_sem.at[0], device_id={"k": z * PLANE + peer}, device_id_type=MESH).start()
        return carry

    lax.fori_loop(1, PLANE, send_tables, 0)
    for off in (1, 2, 3):
        pltpu.make_async_remote_copy(
            src_ref=crow_ref, dst_ref=cb.at[pl.ds(z, 1)], send_sem=csend_sem.at[0], recv_sem=crecv_sem.at[0],
            device_id=z_dev(off), device_id_type=MESH).start()

    line_near(0)
    side_near(0, 0)
    line_near(1)
    line_far(0)

    tloc.wait()
    cloc.wait()
    bytes_wait(tblb.at[pl.ds(0, 2 * (PLANE - 1))], trecv_sem.at[0])
    bytes_wait(cb.at[pl.ds(0, 3)], crecv_sem.at[0])
    to_smem = pltpu.make_async_copy(tblb, tbl_s, smem_sem.at[0])
    to_smem.start()

    side_near(0, 1)
    side_near(0, 3)
    line_far(1)

    codes = jnp.concatenate([tblb[pl.ds(2 * p + 1, 1), 0] for p in range(PLANE)], axis=0)
    wanted = jnp.sum(cb[...], axis=0)
    row = lax.broadcasted_iota(jnp.int32, codes.shape, 0)
    lane = lax.broadcasted_iota(jnp.int32, codes.shape, 1)
    index = row * SLOTS + 2 * ((lane % 64) // n_own) + lane // 64
    hit = jnp.where(codes == wanted, index - NOSLOT, 0)
    selv[...] = NOSLOT + jnp.where(hit != 0, hit, pltpu.roll(hit, 64, 1))

    side_near(0, 2)
    for j in range(4):
        side_far(0, order_of(j))
    to_smem.wait()
    to_sel = pltpu.make_async_copy(selv, sel_s, sel_sem.at[0])
    to_sel.start()

    def compute(ch, core, df, ds, prod):
        slot = slot_of(core, df, ds)
        lhs = held_a[ch][core, slot].reshape(4 * chunk_rows, -1)
        for pair in (0, 1):
            rhs = jnp.concatenate([held_b[core, slot, 2 * pair], held_b[core, slot, 2 * pair + 1]], axis=1)
            res = jnp.dot(lhs, rhs, preferred_element_type=jnp.float32)
            for a in range(4):
                for b in (0, 1):
                    prod[a * 4 + 2 * pair + b] = res[a * chunk_rows:(a + 1) * chunk_rows, b * cols:(b + 1) * cols]
        src = slot * 2 + core
        for j in range(SLOTS):
            total = prod[tbl_s[2 * src, 0, 4 * j]]
            for u in (1, 2, 3):
                total = total + prod[tbl_s[2 * src, 0, 4 * j + u]]
            parts[ch][src * SLOTS + j] = total.astype(jnp.bfloat16).astype(jnp.float32)

    def both(ch, df, ds, first=True):
        slot = slot_of(1 - c, df, ds)
        if ch == 0:
            bytes_wait(whole(0, 1 - c, slot), sib_sem.at[0, slot])
        bytes_wait(whole(1 + ch, 1 - c, slot), sib_sem.at[1 + ch, slot])
        compute(ch, c, df, ds, prods[0])
        compute(ch, 1 - c, df, ds, prods[1])

    def loop(n, body):
        def run(j, carry):
            body(j)
            return carry
        lax.fori_loop(0, n, run, 0)

    def block_sum(ch, zz, t):
        def add(p8, total):
            for u in range(8):
                total = total + parts[ch][sel_s[p8 * 8 + u, zz * n_own + t]]
            return total
        return lax.fori_loop(0, PLANE // 8, add, zero)

    z_up, z_two, z_down = (z + 1) % 4, (z + 2) % 4, (z + 3) % 4

    def z_push(ch, zz, t, dst, recv, off):
        pltpu.make_async_remote_copy(
            src_ref=acc[ch].at[zz, pl.ds(t, GROUP)], dst_ref=dst, send_sem=rs_send.at[ch], recv_sem=recv,
            device_id=z_dev(off), device_id_type=MESH).start()

    def far(ch):
        def body(g):
            t = g * GROUP
            for u in range(GROUP):
                acc[ch][z_two, t + u] = block_sum(ch, z_two, t + u)
                acc[ch][z_two, t + half_own + u] = block_sum(ch, z_two, t + half_own + u)
            z_push(ch, z_two, t, opp[ch].at[0, pl.ds(t, GROUP)], opp_sem.at[ch, 0, g], 1)
            z_push(ch, z_two, t + half_own, opp[ch].at[1, pl.ds(t, GROUP)], opp_sem.at[ch, 1, g], 3)
        loop(n_grp, body)

    def near(ch):
        def body(g):
            t = g * GROUP
            for u in range(GROUP):
                acc[ch][z_up, t + half_own + u] = block_sum(ch, z_up, t + half_own + u)
                acc[ch][z_down, t + u] = block_sum(ch, z_down, t + u)
            z_push(ch, z_up, t + half_own, fin[ch].at[0, pl.ds(t + half_own, GROUP)], fin_sem.at[ch, 0, g + n_grp], 1)
            z_push(ch, z_down, t, fin[ch].at[1, pl.ds(t, GROUP)], fin_sem.at[ch, 1, g], 3)
        loop(n_grp, body)

    def combined(ch):
        def body(g):
            t = g * GROUP
            up = [block_sum(ch, z_up, t + u) for u in range(GROUP)]
            for u in range(GROUP):
                acc[ch][z_up, t + u] = up[u]
            down = [block_sum(ch, z_down, t + half_own + u) for u in range(GROUP)]
            for u in range(GROUP):
                acc[ch][z_down, t + half_own + u] = down[u]
            bytes_wait(opp[ch].at[0, pl.ds(t, GROUP)], opp_sem.at[ch, 0, g])
            bytes_wait(opp[ch].at[1, pl.ds(t, GROUP)], opp_sem.at[ch, 1, g])
            for u in range(GROUP):
                acc[ch][z_up, t + u] += opp[ch][0, t + u]
                acc[ch][z_down, t + half_own + u] += opp[ch][1, t + u]
            z_push(ch, z_up, t, fin[ch].at[0, pl.ds(t, GROUP)], fin_sem.at[ch, 0, g], 1)
            z_push(ch, z_down, t + half_own, fin[ch].at[1, pl.ds(t + half_own, GROUP)], fin_sem.at[ch, 1, g + n_grp], 3)
        loop(n_grp, body)

    def mine(ch):
        def body(t):
            acc[ch][z, t] = block_sum(ch, z, t)
        loop(n_own, body)

    def finish(ch):
        def body(g):
            for gg in (g, g + n_grp):
                t = gg * GROUP
                for side in (0, 1):
                    bytes_wait(fin[ch].at[side, pl.ds(t, GROUP)], fin_sem.at[ch, side, gg])
                for u in range(GROUP):
                    out_ref[t + u, pl.ds(ch * chunk_rows, chunk_rows)] = (
                        acc[ch][z, t + u] + (fin[ch][0, t + u] + fin[ch][1, t + u]))
        loop(n_grp, body)

    def step_a(j):
        df = order_of(j)
        side_near(1, df)
        both(0, df, 0)
    loop(4, step_a)
    to_s(2, my_slot)
    to_sibling(2, my_slot)
    line_near(2)
    line_far(2)

    def step_b(j):
        df = order_of(j)
        side_far(1, df)
        both(0, df, 1)
        both(0, df, 3)
    loop(4, step_b)

    def step_c(j):
        df = order_of(j)
        side_near(2, df)
        both(0, df, 2)
    loop(4, step_c)
    to_sel.wait()

    far(0)
    near(0)

    def step_d(j):
        df = order_of(j)
        side_far(2, df)
        both(1, df, 0)
        both(1, df, 1)
        both(1, df, 3)
    loop(4, step_d)

    def step_e(j):
        both(1, order_of(j), 2)
    loop(4, step_e)

    combined(0)
    far(1)
    near(1)
    mine(0)
    finish(0)
    combined(1)
    mine(1)
    finish(1)

    for k in range(1 + CHUNKS):
        bytes_wait(pieces[k].at[0, pl.ds(0, 3)], f_sem.at[k])
        bytes_wait(pieces[k].at[0, pl.ds(0, 12)], s_sem.at[k])
        bytes_wait(pieces[k].at[0], d_sem.at[k])
    bytes_wait(tblb.at[pl.ds(0, 2 * (PLANE - 1))], tsend_sem.at[0])
    bytes_wait(cb.at[pl.ds(0, 3)], csend_sem.at[0])
    for ch in range(CHUNKS):
        bytes_wait(acc[ch].at[pl.ds(0, 3)], rs_send.at[ch])


def tables(pairs, coords, cidx, z):
    n_own = cidx.shape[0]
    pid = jnp.where(pairs[..., 0] >= 0, pairs[..., 0] * 4 + pairs[..., 1], NOPAIR)
    pid = pid.reshape(4, RING, PLANE, 2).transpose(2, 1, 3, 0).reshape(PLANE, 1, 4 * SLOTS)
    pid = jnp.pad(pid, ((0, 0), (0, 0), (0, 128 - 4 * SLOTS)))
    code = jnp.where(coords[:, 0] >= 0, coords[:, 0] * 256 + coords[:, 1], -1)
    code = code.reshape(RING, PLANE, 2).transpose(1, 2, 0)
    code = jnp.broadcast_to(code[..., None], (PLANE, 2, RING, n_own)).reshape(PLANE, 1, 128)
    tbl = jnp.concatenate([pid, code], axis=1).reshape(2 * PLANE, 1, 128)
    own = cidx[:, 0] * 256 + cidx[:, 1]
    at = jnp.arange(RING)[:, None] == z
    crow = jnp.broadcast_to(jnp.where(at, own[None, :], 0)[None], (2, RING, n_own)).reshape(1, 1, 128)
    return tbl, crow


def solution(mesh):
    dev_spec = P(("batch", "k"))

    def per_device(a_loc, b_loc, pair_loc, coord_loc, cidx_loc):
        a, b, cidx = a_loc[0], b_loc[0], cidx_loc[0]
        n_own = cidx.shape[0]
        rows, depth, cols = a.shape[1], a.shape[2], b.shape[2]
        cr = rows // CHUNKS
        tbl, crow = tables(pair_loc[0], coord_loc[0], cidx, lax.axis_index("k") // PLANE)
        f32, i32, bf16 = jnp.float32, jnp.int32, jnp.bfloat16
        dma = pltpu.SemaphoreType.DMA
        out = pl.pallas_call(
            kernel,
            out_shape=jax.ShapeDtypeStruct((n_own, rows, cols), f32),
            in_specs=[pl.BlockSpec(memory_space=pl.ANY)] * 4,
            out_specs=pl.BlockSpec(memory_space=pltpu.VMEM),
            scratch_shapes=[
                pltpu.VMEM((2, LINES, 4, depth, cols), bf16),
                [pltpu.VMEM((2, LINES, 4, cr, depth), bf16) for _ in range(CHUNKS)],
                [pltpu.VMEM((NOPAIR + 1, cr, cols), f32) for _ in range(2)],
                [pltpu.VMEM((NOSLOT + 1, cr, cols), f32) for _ in range(CHUNKS)],
                [pltpu.VMEM((RING, n_own, cr, cols), f32) for _ in range(CHUNKS)],
                [pltpu.VMEM((2, n_own // 2, cr, cols), f32) for _ in range(CHUNKS)],
                [pltpu.VMEM((2, n_own, cr, cols), f32) for _ in range(CHUNKS)],
                pltpu.VMEM((2 * PLANE, 1, 128), i32),
                pltpu.VMEM((RING, 1, 128), i32),
                pltpu.VMEM((PLANE, 128), i32),
                pltpu.SMEM((2 * PLANE, 1, 128), i32),
                pltpu.SMEM((PLANE, 128), i32),
                dma((1 + CHUNKS,)),
                dma((1 + CHUNKS, LINES, 2)), dma((1 + CHUNKS, LINES)),
                dma((1 + CHUNKS,)), dma((1 + CHUNKS,)), dma((1 + CHUNKS,)),
                dma((1,)), dma((1,)), dma((1,)), dma((1,)), dma((2,)), dma((1,)), dma((1,)),
                dma((CHUNKS,)), dma((CHUNKS, 2, n_own // 2 // GROUP)), dma((CHUNKS, 2, n_own // GROUP)),
            ],
            compiler_params=pltpu.CompilerParams(collective_id=0, has_side_effects=True,
                                                 vmem_limit_bytes=60 * 1024 * 1024),
        )(a, b, tbl, crow)
        return out[None]

    return jax.shard_map(per_device, mesh=mesh, in_specs=(dev_spec,) * 5, out_specs=dev_spec, check_vma=False)
```

time: 304 us -> 81.8 us (0.27)
  waiting for transfers between devices: 112 us -> 0 us
  local copies, waits for them, and re-layouts: 91.8 us -> 5.35 us
  Pallas kernels: 0 us -> 75.6 us
  matrix products: 68.1 us -> 0 us
  starting transfers between devices: 22.2 us -> 0 us
  other arithmetic: 6.91 us -> 0.14 us
    all_to_all x2 -> x0, waiting for transfers between devices: 112 us -> none  [the longest x1 112 us: per_device(): recv_blocks = lax.all_to_all(sent_blocks, 'k', 0, 0, tiled=True)]
    pallas_call x0 -> x1, Pallas kernels: none -> 75.6 us  [per_device(): pl.pallas_call(kernel, out_shape=jax.ShapeDtypeStruct((n_own, rows, cols)...]
    gather x8 -> x0, local copies, waits for them, and re-layouts: 69.7 us -> none  [the longest x4 36.8 us: pair_step(): right_ops = jnp.take(b_blocks, jnp.maximum(pair_rank[:, 1], 0), axis=0)]
    dot_general x5 -> x0, matrix products: 68.1 us -> none  [the longest x4 66.8 us: pair_step(): jnp.einsum('sab,sbc->sac', left_ops, right_ops, preferred_element_type=jn...]
    all_to_all x2 -> x0, starting transfers between devices: 22.2 us -> none  [the longest x1 12 us: per_device(): lax.all_to_all(coord_loc[0].reshape(groups, seg_len, 2), 'k', 0, 0, tiled...]
    all_to_all x2 -> x0, local copies, waits for them, and re-layouts: 8.21 us -> none  [the longest x1 7.3 us: per_device(): recv_blocks = lax.all_to_all(sent_blocks, 'k', 0, 0, tiled=True)]
    reshape x2 -> x1, local copies, waits for them, and re-layouts: 8.18 us -> 0.6 us  [tables(): jnp.broadcast_to(jnp.where(at, own[None, :], 0)[None], (2, RING, n_own))]
    convert_element_type x1 -> x0, other arithmetic: 6.65 us -> none  [per_device(): scan_out[0].astype(jnp.bfloat16)]
  transfers between devices with their start and end apart: 2 -> 0, of which waited for: 1 -> 0; matrix products, arithmetic and copies ran while one was open for 52% -> 0% of each run, Pallas kernels for 0% -> 0%
where the time goes in v2:
time: 81.8 us; the launch traced here: 81.1 us
  Pallas kernels  75.6 us (92%)
  local copies, waits for them, and re-layouts  5.35 us (7%)
    pallas_call x1, Pallas kernels, per_device(): pl.pallas_call(kernel, out_shape=jax.ShapeDtypeStruct((n_own, rows, cols)...  75.6 us
    unnamed x7, local copies, waits for them, and re-layouts  3.57 us

profile of v2, /device:TPU:1, one launch (start us, length us, event | category | flops | bytes accessed | tf_op | source)
XLA Modules:
  0.0 81.1 jit_solution(15401556223061686925)
XLA Ops:
  0.0 0.0 copy-start.2
  0.0 0.7 copy-done.2
  0.7 0.0 copy-start.1
  0.7 0.0 copy-start
  0.7 0.1 broadcast_select_fusion
  0.8 0.6 copy-done.1
  1.4 0.6 reshape.81.crow_ref
  2.0 0.0 copy-done
  2.0 0.1 select_n.32
  2.1 0.1 copy.20
  2.3 0.1 copy.18
  2.4 0.1 copy.19
  2.5 0.7 copy.21
  3.2 75.6 %shard_map.55 = f32[16,128,128]{2,1,0:T(8,128)} custom-call(bf16[4,128,128]{2,1,0:T(8,128)(2,1)} %bitcast.19, bf16[4,128,128]{2,1,0:T(8,128)(2,1)} %bitcast.20, s32[64,1,128]{2,1,0:T(1,128)} %bitcast.21, s32[1,1,128]{2,1,0:T(1,128)} %reshape.81.crow_ref), custom_call_target="tpu_custom_call" | custom-call | tf_op jit(solution)/shard_map/pallas_call | solution.py:379
  78.8 2.3 %copy.23 = f32[1,16,128,128]{3,2,1,0:T(8,128)} copy(f32[1,16,128,128]{3,2,1,0:T(8,128)} %bitcast.15) | data formatting | bytes 2097152
  (7 shorter events, 0.1 us)
Async XLA Ops:
  0.0 0.7 copy-start.2
  0.7 0.7 copy-start.1
  0.7 1.3 %copy-start = (s32[1,4,256,2]{2,3,1,0:T(2,128)S(1)}, s32[1,4,256,2]{2,3,1,0:T(2,128)}, u32[]{:S(2)}) copy-start(s32[1,4,256,2]{2,3,1,0:T(2,128)} %param.7) | copy-start | bytes 24580

commit v3 on v2

--- a/solution.py
+++ b/solution.py
@@ -20,9 +20,9 @@
     return j + (j // 2) * (1 - 2 * (j % 2))
 
 
-def kernel(a_ref, b_ref, tbl_ref, crow_ref, out_ref, held_b, held_a, prods, parts, acc, opp, fin, tblb, cb, selv,
-           tbl_s, sel_s, local_sem, own_sem, sib_sem, f_sem, s_sem, d_sem, tsend_sem, trecv_sem, csend_sem, crecv_sem,
-           tloc_sem, smem_sem, sel_sem, rs_send, opp_sem, fin_sem):
+def kernel(a_ref, b_ref, pairs_ref, coords_ref, cidx_ref, out_ref, held_b, held_a, held_t, prods, parts, acc, opp, fin,
+           cb, tblv, selv, tbl_s, sel_s, local_sem, own_sem, sib_sem, f_sem, s_sem, d_sem, csend_sem, crecv_sem,
+           smem_sem, sel_sem, rs_send, opp_sem, fin_sem):
     me = lax.axis_index("k")
     z = me // PLANE
     d = me % PLANE
@@ -56,16 +56,13 @@
 
     barrier = pltpu.get_barrier_semaphore()
 
-    def greet(r, carry):
-        pl.semaphore_signal(barrier, inc=1, device_id={"k": z * PLANE + (d + r) % PLANE}, device_id_type=MESH)
-        return carry
-
-    lax.fori_loop(1, PLANE, greet, 0)
-    for off in (1, 2, 3):
-        pl.semaphore_signal(barrier, inc=1, device_id=z_dev(off), device_id_type=MESH)
+    for peer in (f_dev(1), f_dev(3), s_dev(1), s_dev(3), sibling, z_dev(1), z_dev(3)):
+        pl.semaphore_signal(barrier, inc=1, device_id=peer, device_id_type=MESH)
 
     my_slot = y * 4 + x
-    pieces = [held_b] + list(held_a)
+    z_up, z_two, z_down = (z + 1) % 4, (z + 2) % 4, (z + 3) % 4
+    pieces = [held_b] + list(held_a) + [held_t]
+    tab = 1 + CHUNKS
 
     loads = [pltpu.make_async_copy(b_ref, held_b.at[c, my_slot], local_sem.at[0])]
     for ch in range(CHUNKS):
@@ -73,24 +70,34 @@
                                            local_sem.at[1 + ch]))
     for cp in loads:
         cp.start()
-    tloc = pltpu.make_async_copy(tbl_ref.at[pl.ds(2 * d, 2)], tblb.at[pl.ds(2 * d, 2)], tloc_sem.at[0])
-    cloc = pltpu.make_async_copy(crow_ref, cb.at[pl.ds(z, 1)], tloc_sem.at[1])
-    tloc.start()
-    cloc.start()
-
     zero = jnp.zeros((chunk_rows, cols), jnp.float32)
     for ref in prods:
         ref[NOPAIR] = zero
     for ref in parts:
         ref[NOSLOT] = zero
 
-    pl.semaphore_wait(barrier, PLANE - 1 + 3)
+    def block_code(ij):
+        return jnp.where(ij[0:1] >= 0, ij[0:1] * 256 + ij[1:2], -1)
+
+    code = block_code(coords_ref[...])
+    for h in (0, 1):
+        span = pl.ds(128 * h, 128)
+        for u in range(4):
+            left = pairs_ref[u, 0:1, span]
+            held_t[c, my_slot, h, u:u + 1] = jnp.where(left >= 0, left * 4 + pairs_ref[u, 1:2, span], NOPAIR)
+        held_t[c, my_slot, h, 4:5] = code[:, 128 * h:128 * h + 128]
+        held_t[c, my_slot, h, 5:8] = jnp.zeros((3, 128), jnp.int32)
+    cb[z] = jnp.full((8, 128), -2, jnp.int32)
+    cb[z, 0:1, 0:n_own] = block_code(cidx_ref[...])
+
+    pl.semaphore_wait(barrier, 7)
 
     def whole(k, core, slot):
         return pieces[k].at[core, slot]
 
     def half(k, core, slot, h):
-        return pieces[k].at[core, slot, pl.ds(2 * h, 2)]
+        n_half = pieces[k].shape[2] // 2
+        return pieces[k].at[core, slot, pl.ds(n_half * h, n_half)]
 
     def send(ref, target, send_sem, recv_sem):
         pltpu.make_async_remote_copy(src_ref=ref, dst_ref=ref, send_sem=send_sem, recv_sem=recv_sem,
@@ -143,56 +150,90 @@
         got_halves(k, slot)
         to_sibling(k, slot)
 
-    for k in range(1 + CHUNKS):
-        loads[k].wait()
-        to_f(k, my_slot)
-        if k < 2:
-            to_s(k, my_slot)
-            to_sibling(k, my_slot)
-
-    def send_tables(r, carry):
-        peer = (d + r) % PLANE
+    loads[0].wait()
+    to_f(0, my_slot)
+    to_s(0, my_slot)
+    to_sibling(0, my_slot)
+    to_f(tab, my_slot)
+    to_s(tab, my_slot)
+    to_sibling(tab, my_slot)
+
+    def push_codes(row, off):
         pltpu.make_async_remote_copy(
-            src_ref=tbl_ref.at[pl.ds(2 * peer, 2)], dst_ref=tblb.at[pl.ds(2 * d, 2)], send_sem=tsend_sem.at[0],
-            recv_sem=trecv_sem.at[0], device_id={"k": z * PLANE + peer}, device_id_type=MESH).start()
+            src_ref=cb.at[row], dst_ref=cb.at[row], send_sem=csend_sem.at[0], recv_sem=crecv_sem.at[row],
+            device_id=z_dev(off), device_id_type=MESH).start()
+
+    push_codes(z, 1)
+    push_codes(z, 3)
+    loads[1].wait()
+    to_f(1, my_slot)
+    to_s(1, my_slot)
+    to_sibling(1, my_slot)
+    loads[2].wait()
+
+    line_near(0)
+    line_near(tab)
+    side_near(0, 0)
+    side_near(tab, 0)
+    line_near(1)
+    side_near(1, 0)
+    line_far(tab)
+    line_far(0)
+    line_far(1)
+    bytes_wait(cb.at[z_down], crecv_sem.at[z_down])
+    push_codes(z_down, 1)
+    side_near(tab, 1)
+    side_near(0, 1)
+    side_near(tab, 3)
+    side_near(tab, 2)
+    side_near(0, 3)
+    for j in range(4):
+        side_far(tab, order_of(j))
+    side_far(0, 0)
+
+    lane = lax.broadcasted_iota(jnp.int32, (8, 128), 1)
+    shift = 2 * PLANE * 2 - 2 * d
+
+    def pick(slot, tables):
+        picked = []
+        for core, table in enumerate(tables):
+            for h in (0, 1):
+                moved = pltpu.roll(held_t[core, slot, h], (shift + 4 * slot + 2 * h) % 128, 1)
+                table = jnp.where((lane % 64) // 2 == 2 * slot + h, moved, table)
+            picked.append(table)
+        return tuple(picked)
+
+    def sib_tables(slot, carry):
+        bytes_wait(whole(tab, 1 - c, slot), sib_sem.at[tab, slot])
         return carry
 
-    lax.fori_loop(1, PLANE, send_tables, 0)
-    for off in (1, 2, 3):
-        pltpu.make_async_remote_copy(
-            src_ref=crow_ref, dst_ref=cb.at[pl.ds(z, 1)], send_sem=csend_sem.at[0], recv_sem=crecv_sem.at[0],
-            device_id=z_dev(off), device_id_type=MESH).start()
-
-    line_near(0)
-    side_near(0, 0)
-    line_near(1)
-    line_far(0)
-
-    tloc.wait()
-    cloc.wait()
-    bytes_wait(tblb.at[pl.ds(0, 2 * (PLANE - 1))], trecv_sem.at[0])
-    bytes_wait(cb.at[pl.ds(0, 3)], crecv_sem.at[0])
-    to_smem = pltpu.make_async_copy(tblb, tbl_s, smem_sem.at[0])
+    lax.fori_loop(0, LINES, sib_tables, 0)
+    none = jnp.zeros((8, 128), jnp.int32)
+    picked = lax.fori_loop(0, LINES, pick, (none, none))
+    for core in (0, 1):
+        tblv[core] = picked[core]
+
+    sub = lax.broadcasted_iota(jnp.int32, (n_own, 128), 0)
+    lane = lax.broadcasted_iota(jnp.int32, (n_own, 128), 1)
+    for row in (z_up, z_two):
+        bytes_wait(cb.at[row], crecv_sem.at[row])
+    wanted = jnp.zeros((n_own, 128), jnp.int32)
+    for zz in range(RING):
+        column = jnp.where(sub == lane, jnp.broadcast_to(cb[zz, 0:1], (n_own, 128)), 0)
+        for bit in range(7):
+            column = column + pltpu.roll(column, 1 << bit, 1)
+        wanted = jnp.where(2 * (lane // 2 % 2) + lane // 64 == zz, column, wanted)
+    for core in (0, 1):
+        source = (lane % 64 // 4) * 2 + core
+        index = source * SLOTS + 2 * (2 * (lane // 2 % 2) + lane // 64) + lane % 2
+        hit = jnp.where(jnp.broadcast_to(picked[core][4:5], (n_own, 128)) == wanted, index - NOSLOT, 0)
+        selv[core] = NOSLOT + jnp.where(hit != 0, hit, pltpu.roll(hit, 127, 1))
+    to_smem = pltpu.make_async_copy(tblv, tbl_s, smem_sem.at[0])
+    to_sel = pltpu.make_async_copy(selv, sel_s, sel_sem.at[0])
     to_smem.start()
-
-    side_near(0, 1)
-    side_near(0, 3)
-    line_far(1)
-
-    codes = jnp.concatenate([tblb[pl.ds(2 * p + 1, 1), 0] for p in range(PLANE)], axis=0)
-    wanted = jnp.sum(cb[...], axis=0)
-    row = lax.broadcasted_iota(jnp.int32, codes.shape, 0)
-    lane = lax.broadcasted_iota(jnp.int32, codes.shape, 1)
-    index = row * SLOTS + 2 * ((lane % 64) // n_own) + lane // 64
-    hit = jnp.where(codes == wanted, index - NOSLOT, 0)
-    selv[...] = NOSLOT + jnp.where(hit != 0, hit, pltpu.roll(hit, 64, 1))
-
-    side_near(0, 2)
-    for j in range(4):
-        side_far(0, order_of(j))
+    to_sel.start()
     to_smem.wait()
-    to_sel = pltpu.make_async_copy(selv, sel_s, sel_sem.at[0])
-    to_sel.start()
+    to_sel.wait()
 
     def compute(ch, core, df, ds, prod):
         slot = slot_of(core, df, ds)
@@ -205,9 +246,10 @@
                     prod[a * 4 + 2 * pair + b] = res[a * chunk_rows:(a + 1) * chunk_rows, b * cols:(b + 1) * cols]
         src = slot * 2 + core
         for j in range(SLOTS):
-            total = prod[tbl_s[2 * src, 0, 4 * j]]
+            at_lane = 64 * (j // 2 % 2) + 4 * slot + 2 * (j // 4) + j % 2
+            total = prod[tbl_s[core, 0, at_lane]]
             for u in (1, 2, 3):
-                total = total + prod[tbl_s[2 * src, 0, 4 * j + u]]
+                total = total + prod[tbl_s[core, u, at_lane]]
             parts[ch][src * SLOTS + j] = total.astype(jnp.bfloat16).astype(jnp.float32)
 
     def both(ch, df, ds, first=True):
@@ -225,13 +267,13 @@
         lax.fori_loop(0, n, run, 0)
 
     def block_sum(ch, zz, t):
+        base = 64 * (zz % 2) + 2 * (zz // 2)
+
         def add(p8, total):
             for u in range(8):
-                total = total + parts[ch][sel_s[p8 * 8 + u, zz * n_own + t]]
+                total = total + parts[ch][sel_s[u % 2, t, base + 4 * (p8 * 4 + u // 2)]]
             return total
         return lax.fori_loop(0, PLANE // 8, add, zero)
-
-    z_up, z_two, z_down = (z + 1) % 4, (z + 2) % 4, (z + 3) % 4
 
     def z_push(ch, zz, t, dst, recv, off):
         pltpu.make_async_remote_copy(
@@ -292,44 +334,53 @@
                         acc[ch][z, t + u] + (fin[ch][0, t + u] + fin[ch][1, t + u]))
         loop(n_grp, body)
 
-    def step_a(j):
-        df = order_of(j)
-        side_near(1, df)
-        both(0, df, 0)
-    loop(4, step_a)
-    to_s(2, my_slot)
-    to_sibling(2, my_slot)
-    line_near(2)
+    def at(n, step, *events):
+        @pl.when(n == step)
+        def _():
+            for event in events:
+                event()
+
+    def step_a(n):
+        at(n, 0, lambda: side_near(1, 1))
+        at(n, 1, lambda: side_near(1, 3))
+        at(n, 2, lambda: side_far(1, 0), lambda: to_f(2, my_slot), lambda: to_s(2, my_slot),
+           lambda: to_sibling(2, my_slot))
+        at(n, 5, lambda: side_near(0, 2))
+        at(n, 7, lambda: side_near(1, 2))
+        at(n, 9, lambda: side_far(0, 1))
+        at(n, 11, lambda: side_far(0, 3))
+        m = n % 3
+        both(0, order_of(n // 3), m + m // 2)
+    loop(12, step_a)
+
+    def step_b(j):
+        at(j, 0, lambda: line_near(2))
+        at(j, 1, lambda: side_far(1, 1))
+        at(j, 2, lambda: side_far(1, 3))
+        at(j, 3, lambda: side_far(0, 2), lambda: side_far(1, 2))
+        both(0, order_of(j), 2)
+    loop(4, step_b)
+    side_near(2, 0)
     line_far(2)
-
-    def step_b(j):
-        df = order_of(j)
-        side_far(1, df)
-        both(0, df, 1)
-        both(0, df, 3)
-    loop(4, step_b)
-
-    def step_c(j):
-        df = order_of(j)
-        side_near(2, df)
-        both(0, df, 2)
-    loop(4, step_c)
-    to_sel.wait()
 
     far(0)
     near(0)
 
+    def step_c(n):
+        at(n, 0, lambda: side_near(2, 1))
+        at(n, 1, lambda: side_near(2, 3))
+        at(n, 2, lambda: side_far(2, 0))
+        at(n, 3, lambda: side_near(2, 2))
+        at(n, 5, lambda: side_far(2, 1))
+        at(n, 6, lambda: side_far(2, 3))
+        at(n, 8, lambda: side_far(2, 2))
+        m = n % 3
+        both(1, order_of(n // 3), m + m // 2)
+    loop(12, step_c)
+
     def step_d(j):
-        df = order_of(j)
-        side_far(2, df)
-        both(1, df, 0)
-        both(1, df, 1)
-        both(1, df, 3)
+        both(1, order_of(j), 2)
     loop(4, step_d)
-
-    def step_e(j):
-        both(1, order_of(j), 2)
-    loop(4, step_e)
 
     combined(0)
     far(1)
@@ -340,69 +391,54 @@
     mine(1)
     finish(1)
 
-    for k in range(1 + CHUNKS):
+    for k in range(2 + CHUNKS):
         bytes_wait(pieces[k].at[0, pl.ds(0, 3)], f_sem.at[k])
         bytes_wait(pieces[k].at[0, pl.ds(0, 12)], s_sem.at[k])
         bytes_wait(pieces[k].at[0], d_sem.at[k])
-    bytes_wait(tblb.at[pl.ds(0, 2 * (PLANE - 1))], tsend_sem.at[0])
     bytes_wait(cb.at[pl.ds(0, 3)], csend_sem.at[0])
     for ch in range(CHUNKS):
         bytes_wait(acc[ch].at[pl.ds(0, 3)], rs_send.at[ch])
 
 
-def tables(pairs, coords, cidx, z):
-    n_own = cidx.shape[0]
-    pid = jnp.where(pairs[..., 0] >= 0, pairs[..., 0] * 4 + pairs[..., 1], NOPAIR)
-    pid = pid.reshape(4, RING, PLANE, 2).transpose(2, 1, 3, 0).reshape(PLANE, 1, 4 * SLOTS)
-    pid = jnp.pad(pid, ((0, 0), (0, 0), (0, 128 - 4 * SLOTS)))
-    code = jnp.where(coords[:, 0] >= 0, coords[:, 0] * 256 + coords[:, 1], -1)
-    code = code.reshape(RING, PLANE, 2).transpose(1, 2, 0)
-    code = jnp.broadcast_to(code[..., None], (PLANE, 2, RING, n_own)).reshape(PLANE, 1, 128)
-    tbl = jnp.concatenate([pid, code], axis=1).reshape(2 * PLANE, 1, 128)
-    own = cidx[:, 0] * 256 + cidx[:, 1]
-    at = jnp.arange(RING)[:, None] == z
-    crow = jnp.broadcast_to(jnp.where(at, own[None, :], 0)[None], (2, RING, n_own)).reshape(1, 1, 128)
-    return tbl, crow
-
-
 def solution(mesh):
     dev_spec = P(("batch", "k"))
 
     def per_device(a_loc, b_loc, pair_loc, coord_loc, cidx_loc):
-        a, b, cidx = a_loc[0], b_loc[0], cidx_loc[0]
-        n_own = cidx.shape[0]
+        a, b = a_loc[0], b_loc[0]
+        pairs, coords, cidx = (jnp.swapaxes(v[0], -1, -2) for v in (pair_loc, coord_loc, cidx_loc))
+        n_own = cidx.shape[1]
         rows, depth, cols = a.shape[1], a.shape[2], b.shape[2]
         cr = rows // CHUNKS
-        tbl, crow = tables(pair_loc[0], coord_loc[0], cidx, lax.axis_index("k") // PLANE)
         f32, i32, bf16 = jnp.float32, jnp.int32, jnp.bfloat16
         dma = pltpu.SemaphoreType.DMA
         out = pl.pallas_call(
             kernel,
             out_shape=jax.ShapeDtypeStruct((n_own, rows, cols), f32),
-            in_specs=[pl.BlockSpec(memory_space=pl.ANY)] * 4,
+            in_specs=[pl.BlockSpec(memory_space=pl.ANY)] * 2 + [pl.BlockSpec(memory_space=pltpu.VMEM)] * 3,
             out_specs=pl.BlockSpec(memory_space=pltpu.VMEM),
             scratch_shapes=[
                 pltpu.VMEM((2, LINES, 4, depth, cols), bf16),
                 [pltpu.VMEM((2, LINES, 4, cr, depth), bf16) for _ in range(CHUNKS)],
+                pltpu.VMEM((2, LINES, 2, 8, 128), i32),
                 [pltpu.VMEM((NOPAIR + 1, cr, cols), f32) for _ in range(2)],
                 [pltpu.VMEM((NOSLOT + 1, cr, cols), f32) for _ in range(CHUNKS)],
                 [pltpu.VMEM((RING, n_own, cr, cols), f32) for _ in range(CHUNKS)],
                 [pltpu.VMEM((2, n_own // 2, cr, cols), f32) for _ in range(CHUNKS)],
                 [pltpu.VMEM((2, n_own, cr, cols), f32) for _ in range(CHUNKS)],
-                pltpu.VMEM((2 * PLANE, 1, 128), i32),
-                pltpu.VMEM((RING, 1, 128), i32),
-                pltpu.VMEM((PLANE, 128), i32),
-                pltpu.SMEM((2 * PLANE, 1, 128), i32),
-                pltpu.SMEM((PLANE, 128), i32),
+                pltpu.VMEM((RING, 8, 128), i32),
+                pltpu.VMEM((2, 8, 128), i32),
+                pltpu.VMEM((2, n_own, 128), i32),
+                pltpu.SMEM((2, 8, 128), i32),
+                pltpu.SMEM((2, n_own, 128), i32),
                 dma((1 + CHUNKS,)),
-                dma((1 + CHUNKS, LINES, 2)), dma((1 + CHUNKS, LINES)),
-                dma((1 + CHUNKS,)), dma((1 + CHUNKS,)), dma((1 + CHUNKS,)),
-                dma((1,)), dma((1,)), dma((1,)), dma((1,)), dma((2,)), dma((1,)), dma((1,)),
+                dma((2 + CHUNKS, LINES, 2)), dma((2 + CHUNKS, LINES)),
+                dma((2 + CHUNKS,)), dma((2 + CHUNKS,)), dma((2 + CHUNKS,)),
+                dma((1,)), dma((RING,)), dma((1,)), dma((1,)),
                 dma((CHUNKS,)), dma((CHUNKS, 2, n_own // 2 // GROUP)), dma((CHUNKS, 2, n_own // GROUP)),
             ],
             compiler_params=pltpu.CompilerParams(collective_id=0, has_side_effects=True,
                                                  vmem_limit_bytes=60 * 1024 * 1024),
-        )(a, b, tbl, crow)
+        )(a, b, pairs, coords, cidx)
         return out[None]
 
     return jax.shard_map(per_device, mesh=mesh, in_specs=(dev_spec,) * 5, out_specs=dev_spec, check_vma=False)

time: 81.8 us -> 81.4 us (level)
  Pallas kernels: 75.6 us -> 78.9 us
  local copies, waits for them, and re-layouts: 5.35 us -> 2.3 us
    pallas_call x1, Pallas kernels: 75.6 us -> 78.9 us  [per_device(): pl.pallas_call(kernel, out_shape=jax.ShapeDtypeStruct((n_own, rows, cols)...]
    unnamed x7 -> x1, local copies, waits for them, and re-layouts: 3.57 us -> 2.3 us
where the time goes in v3:
time: 81.4 us; the launch traced here: 81.2 us
  Pallas kernels  78.9 us (97%)
  local copies, waits for them, and re-layouts  2.3 us (3%)
    pallas_call x1, Pallas kernels, per_device(): pl.pallas_call(kernel, out_shape=jax.ShapeDtypeStruct((n_own, rows, cols)...  78.9 us
    unnamed x1, local copies, waits for them, and re-layouts  2.3 us

profile of v3, /device:TPU:1, one launch (start us, length us, event | category | flops | bytes accessed | tf_op | source)
XLA Modules:
  0.0 81.2 jit_solution(14909266283599470880)
XLA Ops:
  0.0 78.9 %shard_map.55 = f32[16,128,128]{2,1,0:T(8,128)} custom-call(bf16[4,128,128]{2,1,0:T(8,128)(2,1)} %bitcast.13, bf16[4,128,128]{2,1,0:T(8,128)(2,1)} %bitcast.14, s32[4,2,256]{2,1,0:T(2,128)} %bitcast.15, s32[2,256]{1,0:T(2,128)} %bitcast.16, s32[2,16]{1,0:T(2,128)} %bitcast.17), custom_call_target="tpu_custom_call" | custom-call | tf_op jit(solution)/shard_map/pallas_call | solution.py:414
  78.9 2.3 %copy.7 = f32[1,16,128,128]{3,2,1,0:T(8,128)} copy(f32[1,16,128,128]{3,2,1,0:T(8,128)} %bitcast.12) | data formatting | bytes 2097152

commit v4 on v3

--- a/solution.py
+++ b/solution.py
@@ -20,8 +20,8 @@
     return j + (j // 2) * (1 - 2 * (j % 2))
 
 
-def kernel(a_ref, b_ref, pairs_ref, coords_ref, cidx_ref, out_ref, held_b, held_a, held_t, prods, parts, acc, opp, fin,
-           cb, tblv, selv, tbl_s, sel_s, local_sem, own_sem, sib_sem, f_sem, s_sem, d_sem, csend_sem, crecv_sem,
+def kernel(a_ref, b_ref, pairs_hbm, coords_hbm, cidx_hbm, out_ref, pairs_ref, coords_ref, cidx_ref, result, held_b, held_a, held_t, prods, parts, acc, opp, fin,
+           cb, tblv, selv, tbl_s, sel_s, ints_sem, out_sem, local_sem, own_sem, sib_sem, f_sem, s_sem, d_sem, csend_sem, crecv_sem,
            smem_sem, sel_sem, rs_send, opp_sem, fin_sem):
     me = lax.axis_index("k")
     z = me // PLANE
@@ -56,7 +56,7 @@
 
     barrier = pltpu.get_barrier_semaphore()
 
-    for peer in (f_dev(1), f_dev(3), s_dev(1), s_dev(3), sibling, z_dev(1), z_dev(3)):
+    for peer in [sibling] + [dev_of(off) for dev_of in (f_dev, s_dev, z_dev) for off in (2, 1, 3)]:
         pl.semaphore_signal(barrier, inc=1, device_id=peer, device_id_type=MESH)
 
     my_slot = y * 4 + x
@@ -64,11 +64,13 @@
     pieces = [held_b] + list(held_a) + [held_t]
     tab = 1 + CHUNKS
 
+    ints = [pltpu.make_async_copy(src, dst, ints_sem.at[i]) for i, (src, dst) in enumerate(
+        ((pairs_hbm, pairs_ref), (coords_hbm, coords_ref), (cidx_hbm, cidx_ref)))]
     loads = [pltpu.make_async_copy(b_ref, held_b.at[c, my_slot], local_sem.at[0])]
     for ch in range(CHUNKS):
         loads.append(pltpu.make_async_copy(a_ref.at[:, pl.ds(ch * chunk_rows, chunk_rows)], held_a[ch].at[c, my_slot],
                                            local_sem.at[1 + ch]))
-    for cp in loads:
+    for cp in ints + loads:
         cp.start()
     zero = jnp.zeros((chunk_rows, cols), jnp.float32)
     for ref in prods:
@@ -76,6 +78,8 @@
     for ref in parts:
         ref[NOSLOT] = zero
 
+    for cp in ints:
+        cp.wait()
     def block_code(ij):
         return jnp.where(ij[0:1] >= 0, ij[0:1] * 256 + ij[1:2], -1)
 
@@ -90,7 +94,7 @@
     cb[z] = jnp.full((8, 128), -2, jnp.int32)
     cb[z, 0:1, 0:n_own] = block_code(cidx_ref[...])
 
-    pl.semaphore_wait(barrier, 7)
+    pl.semaphore_wait(barrier, 10)
 
     def whole(k, core, slot):
         return pieces[k].at[core, slot]
@@ -150,46 +154,44 @@
         got_halves(k, slot)
         to_sibling(k, slot)
 
-    loads[0].wait()
-    to_f(0, my_slot)
-    to_s(0, my_slot)
-    to_sibling(0, my_slot)
-    to_f(tab, my_slot)
-    to_s(tab, my_slot)
-    to_sibling(tab, my_slot)
-
-    def push_codes(row, off):
+    def t_line(slot):
+        for off in (2, 1, 3):
+            send(whole(tab, c, slot), s_dev(off), s_sem.at[tab], own_sem.at[tab, slot, 0])
+        to_sibling(tab, slot)
+
+    for off in (2, 1, 3):
+        send(whole(tab, c, my_slot), f_dev(off), f_sem.at[tab], own_sem.at[tab, my_slot, 0])
+    t_line(my_slot)
+    for off in (2, 1, 3):
         pltpu.make_async_remote_copy(
-            src_ref=cb.at[row], dst_ref=cb.at[row], send_sem=csend_sem.at[0], recv_sem=crecv_sem.at[row],
+            src_ref=cb.at[z], dst_ref=cb.at[z], send_sem=csend_sem.at[0], recv_sem=crecv_sem.at[z],
             device_id=z_dev(off), device_id_type=MESH).start()
-
-    push_codes(z, 1)
-    push_codes(z, 3)
-    loads[1].wait()
-    to_f(1, my_slot)
-    to_s(1, my_slot)
-    to_sibling(1, my_slot)
+    for k in (0, 1):
+        loads[k].wait()
+        to_f(k, my_slot)
+        to_s(k, my_slot)
+        to_sibling(k, my_slot)
     loads[2].wait()
 
+    for df in (1, 3, 2):
+        slot = slot_of(c, df, 0)
+        got_whole(tab, slot)
+        t_line(slot)
     line_near(0)
-    line_near(tab)
     side_near(0, 0)
-    side_near(tab, 0)
     line_near(1)
     side_near(1, 0)
-    line_far(tab)
+
+    def t_side(n, carry):
+        slot = slot_of(c, n // 3, 1 + n % 3)
+        got_whole(tab, slot)
+        to_sibling(tab, slot)
+        return carry
+
+    lax.fori_loop(0, 12, t_side, 0)
     line_far(0)
     line_far(1)
-    bytes_wait(cb.at[z_down], crecv_sem.at[z_down])
-    push_codes(z_down, 1)
-    side_near(tab, 1)
     side_near(0, 1)
-    side_near(tab, 3)
-    side_near(tab, 2)
-    side_near(0, 3)
-    for j in range(4):
-        side_far(tab, order_of(j))
-    side_far(0, 0)
 
     lane = lax.broadcasted_iota(jnp.int32, (8, 128), 1)
     shift = 2 * PLANE * 2 - 2 * d
@@ -215,7 +217,7 @@
 
     sub = lax.broadcasted_iota(jnp.int32, (n_own, 128), 0)
     lane = lax.broadcasted_iota(jnp.int32, (n_own, 128), 1)
-    for row in (z_up, z_two):
+    for row in (z_up, z_two, z_down):
         bytes_wait(cb.at[row], crecv_sem.at[row])
     wanted = jnp.zeros((n_own, 128), jnp.int32)
     for zz in range(RING):
@@ -232,6 +234,8 @@
     to_sel = pltpu.make_async_copy(selv, sel_s, sel_sem.at[0])
     to_smem.start()
     to_sel.start()
+    side_near(0, 3)
+    side_far(0, 0)
     to_smem.wait()
     to_sel.wait()
 
@@ -323,6 +327,10 @@
             acc[ch][z, t] = block_sum(ch, z, t)
         loop(n_own, body)
 
+    def out_copy(gg):
+        span = pl.ds(gg * GROUP, GROUP)
+        return pltpu.make_async_copy(result.at[span], out_ref.at[span], out_sem.at[gg])
+
     def finish(ch):
         def body(g):
             for gg in (g, g + n_grp):
@@ -330,8 +338,10 @@
                 for side in (0, 1):
                     bytes_wait(fin[ch].at[side, pl.ds(t, GROUP)], fin_sem.at[ch, side, gg])
                 for u in range(GROUP):
-                    out_ref[t + u, pl.ds(ch * chunk_rows, chunk_rows)] = (
+                    result[t + u, pl.ds(ch * chunk_rows, chunk_rows)] = (
                         acc[ch][z, t + u] + (fin[ch][0, t + u] + fin[ch][1, t + u]))
+                if ch == CHUNKS - 1:
+                    out_copy(gg).start()
         loop(n_grp, body)
 
     def at(n, step, *events):
@@ -391,7 +401,11 @@
     mine(1)
     finish(1)
 
-    for k in range(2 + CHUNKS):
+    loop(2 * n_grp, lambda gg: out_copy(gg).wait())
+    bytes_wait(held_t.at[0, pl.ds(0, 3)], f_sem.at[tab])
+    bytes_wait(held_t.at[0, pl.ds(0, 12)], s_sem.at[tab])
+    bytes_wait(held_t.at[0], d_sem.at[tab])
+    for k in range(1 + CHUNKS):
         bytes_wait(pieces[k].at[0, pl.ds(0, 3)], f_sem.at[k])
         bytes_wait(pieces[k].at[0, pl.ds(0, 12)], s_sem.at[k])
         bytes_wait(pieces[k].at[0], d_sem.at[k])
@@ -414,9 +428,11 @@
         out = pl.pallas_call(
             kernel,
             out_shape=jax.ShapeDtypeStruct((n_own, rows, cols), f32),
-            in_specs=[pl.BlockSpec(memory_space=pl.ANY)] * 2 + [pl.BlockSpec(memory_space=pltpu.VMEM)] * 3,
-            out_specs=pl.BlockSpec(memory_space=pltpu.VMEM),
+            in_specs=[pl.BlockSpec(memory_space=pl.ANY)] * 5,
+            out_specs=pl.BlockSpec(memory_space=pl.ANY),
             scratch_shapes=[
+                pltpu.VMEM(pairs.shape, i32), pltpu.VMEM(coords.shape, i32), pltpu.VMEM(cidx.shape, i32),
+                pltpu.VMEM((n_own, rows, cols), f32),
                 pltpu.VMEM((2, LINES, 4, depth, cols), bf16),
                 [pltpu.VMEM((2, LINES, 4, cr, depth), bf16) for _ in range(CHUNKS)],
                 pltpu.VMEM((2, LINES, 2, 8, 128), i32),
@@ -430,7 +446,7 @@
                 pltpu.VMEM((2, n_own, 128), i32),
                 pltpu.SMEM((2, 8, 128), i32),
                 pltpu.SMEM((2, n_own, 128), i32),
-                dma((1 + CHUNKS,)),
+                dma((3,)), dma((n_own // GROUP,)), dma((1 + CHUNKS,)),
                 dma((2 + CHUNKS, LINES, 2)), dma((2 + CHUNKS, LINES)),
                 dma((2 + CHUNKS,)), dma((2 + CHUNKS,)), dma((2 + CHUNKS,)),
                 dma((1,)), dma((RING,)), dma((1,)), dma((1,)),

time: 81.4 us -> 73.8 us (0.907)
  Pallas kernels: 78.9 us -> 71.4 us
    pallas_call x1, Pallas kernels: 78.9 us -> 71.4 us  [per_device(): pl.pallas_call(kernel, out_shape=jax.ShapeDtypeStruct((n_own, rows, cols)...]
where the time goes in v4:
time: 73.8 us; the launch traced here: 73.7 us
  Pallas kernels  71.4 us (97%)
  local copies, waits for them, and re-layouts  2.3 us (3%)
    pallas_call x1, Pallas kernels, per_device(): pl.pallas_call(kernel, out_shape=jax.ShapeDtypeStruct((n_own, rows, cols)...  71.4 us
    unnamed x1, local copies, waits for them, and re-layouts  2.3 us

profile of v4, /device:TPU:1, one launch (start us, length us, event | category | flops | bytes accessed | tf_op | source)
XLA Modules:
  0.0 73.7 jit_solution(514246013294764818)
XLA Ops:
  0.0 71.4 %shard_map.55 = f32[16,128,128]{2,1,0:T(8,128)} custom-call(bf16[4,128,128]{2,1,0:T(8,128)(2,1)} %bitcast.13, bf16[4,128,128]{2,1,0:T(8,128)(2,1)} %bitcast.14, s32[4,2,256]{2,1,0:T(2,128)} %bitcast.15, s32[2,256]{1,0:T(2,128)} %bitcast.16, s32[2,16]{1,0:T(2,128)} %bitcast.17), custom_call_target="tpu_custom_call" | custom-call | tf_op jit(solution)/shard_map/pallas_call | solution.py:428
  71.4 2.3 %copy.7 = f32[1,16,128,128]{3,2,1,0:T(8,128)} copy(f32[1,16,128,128]{3,2,1,0:T(8,128)} %bitcast.12) | data formatting | bytes 2097152

commit v5 on v0

v5 whole, which is shorter than its diff:
```python
import jax
import jax.numpy as jnp
from jax import lax
from jax.experimental import pallas as pl
from jax.experimental.pallas import tpu as pltpu
from jax.sharding import PartitionSpec as P

RING = 4
PLANE = 32
LINES = PLANE // 2
SLOTS = 8
NOPAIR = 16
NOSLOT = PLANE * SLOTS
ROWS = (64, 64)
B, A, TAB = range(3)
XY, XZ = PASSES = range(2)
OWN, NEXT, FAR, PREV = range(RING)
OTHERS = (FAR, NEXT, PREV)
NEAR = (NEXT, PREV)
CHUNKS = len(ROWS)
FIRST = tuple(sum(ROWS[:ch]) for ch in range(CHUNKS))
GROUP = 4
MESH = pl.DeviceIdType.MESH


def order_of(j):
    return j + (j // 2) * (1 - 2 * (j % 2))


def kernel(a_ref, b_ref, pairs_hbm, coords_hbm, cidx_hbm, out_ref, pairs_ref, coords_ref, cidx_ref, result, held_b,
           held_a, held_t, prods, parts, acc, opp, fin, cb, tblv, selv, tbl_s, sel_s, ints_sem, out_sem, local_sem,
           own_sem, sib_sem, f_sem, s_sem, d_sem, csend_sem, crecv_sem, smem_sem, sel_sem, rs_send, opp_sem, fin_sem):
    me = lax.axis_index("k")
    z = me // PLANE
    y = me % PLANE // 8
    x = me % 8 // 2
    c = me % 2
    n_own = out_ref.shape[0]
    half_own = n_own // 2
    n_grp = half_own // GROUP
    cols = out_ref.shape[2]

    def dev(zz, yy, xx, cc):
        return {"k": ((zz * 4 + yy) * 4 + xx) * 2 + cc}

    sibling = dev(z, y, x, 1 - c)

    def f_dev(p, off):
        if p == 0:
            return dev(z, (y + off * c) % 4, (x + off * (1 - c)) % 4, c)
        return dev(z, y, (x + off) % 4, c)

    def s_dev(p, off):
        if p == 0:
            return dev(z, (y + off * (1 - c)) % 4, (x + off * c) % 4, c)
        return dev((z + off) % 4, y, x, c)

    def r_dev(p, off):
        if p == 0:
            return dev((z + off) % 4, y, x, c)
        return dev(z, (y + off) % 4, x, c)

    def slot_of(p, core, df, ds):
        if p == 0:
            sx = (x + df * (1 - core) + ds * core) % 4
            sy = (y + df * core + ds * (1 - core)) % 4
            return sy * 4 + sx
        return (z + ds) % 4 * 4 + (x + df) % 4

    my_slot = (y * 4 + x, z * 4 + x)
    here = (z, y)
    up, two, down = ([(v + off) % 4 for v in here] for off in (1, 2, 3))

    barrier = pltpu.get_barrier_semaphore()
    for peer in [sibling] + [dev_of(0, off) for dev_of in (f_dev, s_dev, r_dev) for off in OTHERS]:
        pl.semaphore_signal(barrier, inc=1, device_id=peer, device_id_type=MESH)

    held = (held_b, held_a, held_t)
    ints = [pltpu.make_async_copy(src, dst, ints_sem.at[i]) for i, (src, dst) in enumerate(
        ((pairs_hbm, pairs_ref), (coords_hbm, coords_ref), (cidx_hbm, cidx_ref)))]
    loads = []
    for p in (1, 0):
        loads.append(pltpu.make_async_copy(b_ref, held_b[p].at[c, my_slot[p]], local_sem.at[2 * p]))
        loads.append(pltpu.make_async_copy(a_ref.at[:, pl.ds(FIRST[p], ROWS[p])], held_a[p].at[c, my_slot[p]],
                                           local_sem.at[2 * p + 1]))
    for cp in ints + loads:
        cp.start()
    for ref in prods:
        ref[NOPAIR] = jnp.zeros(ref.shape[1:], jnp.float32)
    for ref in parts:
        ref[NOSLOT] = jnp.zeros(ref.shape[1:], jnp.float32)

    for cp in ints:
        cp.wait()

    def block_code(ij):
        return jnp.where(ij[0:1] >= 0, ij[0:1] * 256 + ij[1:2], -1)

    code = block_code(coords_ref[...])
    for h in (0, 1):
        span = pl.ds(128 * h, 128)
        for u in range(4):
            left = pairs_ref[u, 0:1, span]
            pid = jnp.where(left >= 0, left * 4 + pairs_ref[u, 1:2, span], NOPAIR)
            for p in PASSES:
                held_t[p][c, my_slot[p], h, u:u + 1] = pid
        for p in PASSES:
            held_t[p][c, my_slot[p], h, 4:5] = code[:, 128 * h:128 * h + 128]
            held_t[p][c, my_slot[p], h, 5:8] = jnp.zeros((3, 128), jnp.int32)
    for p in PASSES:
        cb[p][here[p]] = jnp.full((8, 128), -2, jnp.int32)
        cb[p][here[p], 0:1, 0:n_own] = block_code(cidx_ref[...])

    pl.semaphore_wait(barrier, 10)

    def whole(p, k, core, slot):
        return held[k][p].at[core, slot]

    def half(p, k, core, slot, h):
        n_half = held[k][p].shape[2] // 2
        return held[k][p].at[core, slot, pl.ds(n_half * h, n_half)]

    def send(ref, target, send_sem, recv_sem):
        pltpu.make_async_remote_copy(src_ref=ref, dst_ref=ref, send_sem=send_sem, recv_sem=recv_sem,
                                     device_id=target, device_id_type=MESH).start()

    def bytes_wait(ref, sem):
        pltpu.make_async_copy(ref, ref, sem).wait()

    def to_sibling(p, k, slot):
        send(whole(p, k, c, slot), sibling, d_sem.at[p, k], sib_sem.at[p, k, slot])

    def to_f(p, k, slot, offs=NEAR):
        for off in offs:
            send(whole(p, k, c, slot), f_dev(p, off), f_sem.at[p, k], own_sem.at[p, k, slot, 0])

    def to_s(p, k, slot, offs=NEAR):
        for off in offs:
            send(whole(p, k, c, slot), s_dev(p, off), s_sem.at[p, k], own_sem.at[p, k, slot, 0])

    def got_whole(p, k, slot):
        bytes_wait(whole(p, k, c, slot), own_sem.at[p, k, slot, 0])

    def got_halves(p, k, slot):
        for h in (0, 1):
            bytes_wait(half(p, k, c, slot, h), own_sem.at[p, k, slot, h])

    def line_near(p, k):
        for df, h, off in ((1, 1, 3), (3, 0, 1)):
            slot = slot_of(p, c, df, 0)
            got_whole(p, k, slot)
            send(half(p, k, c, slot, h), f_dev(p, off), f_sem.at[p, k], own_sem.at[p, k, slot, h])
            to_s(p, k, slot)
            to_sibling(p, k, slot)

    def line_far(p, k):
        slot = slot_of(p, c, 2, 0)
        got_halves(p, k, slot)
        to_s(p, k, slot)
        to_sibling(p, k, slot)

    def side_near(df, p, k):
        for ds, h, off in ((1, 1, 3), (3, 0, 1)):
            slot = slot_of(p, c, df, ds)
            got_whole(p, k, slot)
            send(half(p, k, c, slot, h), s_dev(p, off), s_sem.at[p, k], own_sem.at[p, k, slot, h])
            to_sibling(p, k, slot)

    def side_far(df, p, k):
        slot = slot_of(p, c, df, 2)
        got_halves(p, k, slot)
        to_sibling(p, k, slot)

    def t_line(p, slot):
        to_s(p, TAB, slot, OTHERS)
        to_sibling(p, TAB, slot)

    def t_lines(p):
        for df in (1, 3, 2):
            slot = slot_of(p, c, df, 0)
            got_whole(p, TAB, slot)
            t_line(p, slot)

    def t_sides(p):
        def t_side(n, carry):
            slot = slot_of(p, c, n // 3, 1 + n % 3)
            got_whole(p, TAB, slot)
            to_sibling(p, TAB, slot)
            return carry
        lax.fori_loop(0, 12, t_side, 0)

    for p in PASSES:
        to_f(p, TAB, my_slot[p], OTHERS)
        t_line(p, my_slot[p])
        for off in OTHERS:
            pltpu.make_async_remote_copy(
                src_ref=cb[p].at[here[p]], dst_ref=cb[p].at[here[p]], send_sem=csend_sem.at[p],
                recv_sem=crecv_sem.at[p, here[p]], device_id=r_dev(p, off), device_id_type=MESH).start()
    for i, cp in enumerate(loads):
        p, k = 1 - i // 2, i % 2
        cp.wait()
        to_f(p, k, my_slot[p])
        to_s(p, k, my_slot[p])
        to_sibling(p, k, my_slot[p])

    def lane_of(p, slot, col, r):
        if p == 0:
            return 64 * (col % 2) + 4 * slot + 2 * (col // 2) + r
        return 64 * (slot // 8) + 16 * col + 2 * (slot % 8) + r

    def build_tables(p):
        lane = lax.broadcasted_iota(jnp.int32, (8, 128), 1)
        start = me % PLANE * 2 if p == 0 else z % 2 * 64 + x * 4 + c * 2

        def sib_tables(slot, carry):
            bytes_wait(whole(p, TAB, 1 - c, slot), sib_sem.at[p, TAB, slot])
            return carry

        lax.fori_loop(0, LINES, sib_tables, 0)

        def pick(slot, tables):
            picked = []
            for core, table in enumerate(tables):
                if p == 0:
                    for h in (0, 1):
                        moved = pltpu.roll(held_t[p][core, slot, h], (128 - start + 4 * slot + 2 * h) % 128, 1)
                        table = jnp.where(lane % 64 // 2 == 2 * slot + h, moved, table)
                else:
                    shift = (256 - start + 64 * (slot // 8) + 2 * (slot % 8)) % 128
                    moved = pltpu.roll(held_t[p][core, slot, z // 2], shift, 1)
                    mine = lane // 64 * 8 + lane % 16 // 2 == slot
                    table = jnp.where(mine, moved, table)
                picked.append(table)
            return tuple(picked)

        none = jnp.zeros((8, 128), jnp.int32)
        picked = lax.fori_loop(0, LINES, pick, (none, none), unroll=8)
        for core in (0, 1):
            tblv[p][core] = picked[core]
        sub = lax.broadcasted_iota(jnp.int32, (n_own, 128), 0)
        lane = lax.broadcasted_iota(jnp.int32, (n_own, 128), 1)
        if p == 0:
            slot, col = lane % 64 // 4, 2 * (lane // 2 % 2) + lane // 64
        else:
            slot, col = lane // 64 * 8 + lane % 16 // 2, lane % 64 // 16
        for row in (up[p], two[p], down[p]):
            bytes_wait(cb[p].at[row], crecv_sem.at[p, row])
        wanted = jnp.zeros((n_own, 128), jnp.int32)
        for cc in range(RING):
            column = jnp.where(sub == lane, jnp.broadcast_to(cb[p][cc, 0:1], (n_own, 128)), 0)
            for bit in range(7):
                column = column + pltpu.roll(column, 1 << bit, 1)
            wanted = jnp.where(col == cc, column, wanted)
        for core in (0, 1):
            index = (slot * 2 + core) * SLOTS + 2 * col + lane % 2
            hit = jnp.where(jnp.broadcast_to(picked[core][4:5], (n_own, 128)) == wanted, index - NOSLOT, 0)
            selv[p][core] = NOSLOT + jnp.where(hit != 0, hit, pltpu.roll(hit, 127, 1))

    def smem_copies(p):
        return (pltpu.make_async_copy(tblv[p], tbl_s[p], smem_sem.at[p]),
                pltpu.make_async_copy(selv[p], sel_s[p], sel_sem.at[p]))

    def compute(p, core, slot, prod):
        chunk_rows = ROWS[p]
        span = pl.ds(0, chunk_rows)
        lhs = held_a[p][core, slot].reshape(4 * chunk_rows, -1)
        for pair in (0, 1):
            rhs = jnp.concatenate([held_b[p][core, slot, 2 * pair], held_b[p][core, slot, 2 * pair + 1]], axis=1)
            res = jnp.dot(lhs, rhs, preferred_element_type=jnp.float32)
            for a in range(4):
                for b in (0, 1):
                    prod[a * 4 + 2 * pair + b, span] = res[a * chunk_rows:(a + 1) * chunk_rows, b * cols:(b + 1) * cols]
        src = slot * 2 + core
        for j in range(SLOTS):
            at_lane = lane_of(p, slot, j // 2, j % 2)
            total = prod[tbl_s[p][core, 0, at_lane], span]
            for u in (1, 2, 3):
                total = total + prod[tbl_s[p][core, u, at_lane], span]
            parts[p][src * SLOTS + j] = total.astype(jnp.bfloat16).astype(jnp.float32)

    def both(p, df, ds):
        slot = slot_of(p, 1 - c, df, ds)
        for k in (0, 1):
            bytes_wait(whole(p, k, 1 - c, slot), sib_sem.at[p, k, slot])
        compute(p, c, slot_of(p, c, df, ds), prods[0])
        compute(p, 1 - c, slot, prods[1])

    def loop(n, body):
        def run(j, carry):
            body(j)
            return carry
        lax.fori_loop(0, n, run, 0)

    def block_sum(p, col, t):
        total = jnp.zeros((ROWS[p], cols), jnp.float32)
        for i in range(LINES):
            for core in range(2):
                total = total + parts[p][sel_s[p][core, t, lane_of(p, i, col, 0)]]
        return total

    def r_push(p, col, t, dst, recv, off):
        pltpu.make_async_remote_copy(
            src_ref=acc[p].at[col, pl.ds(t, GROUP)], dst_ref=dst, send_sem=rs_send.at[p], recv_sem=recv,
            device_id=r_dev(p, off), device_id_type=MESH).start()

    def sums(p, g, col_of, high):
        def body(i):
            side = i // GROUP
            t = g * GROUP + i % GROUP + half_own * (side * (1 - high) + (1 - side) * high)
            col = col_of(side)
            acc[p][col, t] = block_sum(p, col, t)
        loop(2 * GROUP, body)

    def beside(p):
        return lambda side: (here[p] + 1 + 2 * side) % RING

    def far(p):
        def body(g):
            t = g * GROUP
            sums(p, g, lambda side: two[p], 0)
            r_push(p, two[p], t, opp[p].at[0, pl.ds(t, GROUP)], opp_sem.at[p, 0, g], 1)
            r_push(p, two[p], t + half_own, opp[p].at[1, pl.ds(t, GROUP)], opp_sem.at[p, 1, g], 3)
        loop(n_grp, body)

    def near(p):
        def body(g):
            t = g * GROUP
            sums(p, g, beside(p), 1)
            r_push(p, up[p], t + half_own, fin[p].at[0, pl.ds(t + half_own, GROUP)], fin_sem.at[p, 0, g + n_grp], 1)
            r_push(p, down[p], t, fin[p].at[1, pl.ds(t, GROUP)], fin_sem.at[p, 1, g], 3)
        loop(n_grp, body)

    def combined(p):
        def body(g):
            t = g * GROUP
            sums(p, g, beside(p), 0)
            for side in range(2):
                bytes_wait(opp[p].at[side, pl.ds(t, GROUP)], opp_sem.at[p, side, g])
            for u in range(GROUP):
                acc[p][up[p], t + u] += opp[p][0, t + u]
                acc[p][down[p], t + half_own + u] += opp[p][1, t + u]
            r_push(p, up[p], t, fin[p].at[0, pl.ds(t, GROUP)], fin_sem.at[p, 0, g], 1)
            r_push(p, down[p], t + half_own, fin[p].at[1, pl.ds(t + half_own, GROUP)], fin_sem.at[p, 1, g + n_grp], 3)
        loop(n_grp, body)

    def mine(p):
        def body(t):
            acc[p][here[p], t] = block_sum(p, here[p], t)
        loop(n_own, body)

    def out_copy(gg):
        span = pl.ds(gg * GROUP, GROUP)
        return pltpu.make_async_copy(result.at[span], out_ref.at[span], out_sem.at[gg])

    def finish(p, last):
        def body(g):
            for gg in (g, g + n_grp):
                t = gg * GROUP
                for side in (0, 1):
                    bytes_wait(fin[p].at[side, pl.ds(t, GROUP)], fin_sem.at[p, side, gg])
                for u in range(GROUP):
                    result[t + u, pl.ds(FIRST[p], ROWS[p])] = (
                        acc[p][here[p], t + u] + (fin[p][0, t + u] + fin[p][1, t + u]))
                if last:
                    out_copy(gg).start()
        loop(n_grp, body)

    def at(n, step, *events):
        @pl.when(n == step)
        def _():
            for event, *args in events:
                event(*args)

    t_lines(XZ)
    t_lines(XY)
    line_near(XZ, B)
    side_near(OWN, XZ, B)
    line_near(XZ, A)
    side_near(OWN, XZ, A)
    side_near(OWN, XY, B)
    line_near(XY, B)
    t_sides(XZ)
    side_near(NEXT, XZ, B)
    side_near(OWN, XY, A)
    line_near(XY, A)
    t_sides(XY)
    line_far(XZ, B)
    line_far(XZ, A)
    build_tables(XY)
    side_near(PREV, XZ, B)
    side_far(OWN, XY, B)
    line_far(XY, B)
    build_tables(XZ)
    for p in PASSES:
        for cp in smem_copies(p):
            cp.start()
    side_far(OWN, XZ, B)
    line_far(XY, A)
    for p in PASSES:
        for cp in smem_copies(p):
            cp.wait()

    def step_a(n):
        df = order_of(n)
        both(XY, df, 0)
        both(XZ, df, 0)
        at(n, 0, (side_near, NEXT, XY, B), (side_near, NEXT, XZ, A))
        at(n, 2, (side_near, PREV, XY, B), (side_near, PREV, XZ, A))
        at(n, 3, (side_far, OWN, XY, A), (side_far, OWN, XZ, A))
    loop(4, step_a)

    def step_b(n):
        df = order_of(n // 2)
        ds = 1 + 2 * (n % 2)
        both(XY, df, ds)
        both(XZ, df, ds)
        at(n, 0, (side_near, NEXT, XY, A))
        at(n, 1, (side_near, PREV, XY, A), (side_far, NEXT, XZ, B))
        at(n, 3, (side_near, FAR, XY, B))
        at(n, 4, (side_near, FAR, XY, A))
        at(n, 5, (side_near, FAR, XZ, B), (side_far, NEXT, XY, B), (side_far, PREV, XY, B), (side_far, NEXT, XY, A), (side_near, FAR, XZ, A))
        at(n, 6, (side_far, PREV, XY, A))
        at(n, 7, (side_far, FAR, XY, B), (side_far, FAR, XY, A))
    loop(8, step_b)

    def step_c(n):
        both(XY, order_of(n), 2)
        at(n, 0, (side_far, PREV, XZ, B))
        at(n, 2, (side_far, NEXT, XZ, A))
    loop(4, step_c)
    far(XY)
    side_far(PREV, XZ, A)
    near(XY)
    side_far(FAR, XZ, B)
    side_far(FAR, XZ, A)

    def step_d(n):
        both(XZ, order_of(n), 2)
    loop(4, step_d)
    far(XZ)
    near(XZ)
    combined(XY)
    combined(XZ)
    mine(XY)
    mine(XZ)
    finish(XY, False)
    finish(XZ, True)

    loop(2 * n_grp, lambda gg: out_copy(gg).wait())
    for p in PASSES:
        for k in (0, 1, TAB):
            bytes_wait(held[k][p].at[0, pl.ds(0, 3)], f_sem.at[p, k])
            bytes_wait(held[k][p].at[0, pl.ds(0, 12)], s_sem.at[p, k])
            bytes_wait(held[k][p].at[0], d_sem.at[p, k])
        bytes_wait(cb[p].at[pl.ds(0, 3)], csend_sem.at[p])
        bytes_wait(acc[p].at[pl.ds(0, 3)], rs_send.at[p])


def solution(mesh):
    dev_spec = P(("batch", "k"))

    def per_device(a_loc, b_loc, pair_loc, coord_loc, cidx_loc):
        a, b = a_loc[0], b_loc[0]
        pairs, coords, cidx = (jnp.swapaxes(v[0], -1, -2) for v in (pair_loc, coord_loc, cidx_loc))
        n_own = cidx.shape[1]
        rows, depth, cols = a.shape[1], a.shape[2], b.shape[2]
        assert rows == sum(ROWS)
        f32, i32, bf16 = jnp.float32, jnp.int32, jnp.bfloat16
        dma = pltpu.SemaphoreType.DMA
        out = pl.pallas_call(
            kernel,
            out_shape=jax.ShapeDtypeStruct((n_own, rows, cols), f32),
            in_specs=[pl.BlockSpec(memory_space=pl.ANY)] * 5,
            out_specs=pl.BlockSpec(memory_space=pl.ANY),
            scratch_shapes=[
                pltpu.VMEM(pairs.shape, i32), pltpu.VMEM(coords.shape, i32), pltpu.VMEM(cidx.shape, i32),
                pltpu.VMEM((n_own, rows, cols), f32),
                [pltpu.VMEM((2, LINES, 4, depth, cols), bf16) for cr in ROWS],
                [pltpu.VMEM((2, LINES, 4, cr, depth), bf16) for cr in ROWS],
                [pltpu.VMEM((2, LINES, 2, 8, 128), i32) for cr in ROWS],
                [pltpu.VMEM((NOPAIR + 1, max(ROWS), cols), f32) for _ in range(2)],
                [pltpu.VMEM((NOSLOT + 1, cr, cols), f32) for cr in ROWS],
                [pltpu.VMEM((RING, n_own, cr, cols), f32) for cr in ROWS],
                [pltpu.VMEM((2, n_own // 2, cr, cols), f32) for cr in ROWS],
                [pltpu.VMEM((2, n_own, cr, cols), f32) for cr in ROWS],
                [pltpu.VMEM((RING, 8, 128), i32) for cr in ROWS],
                [pltpu.VMEM((2, 8, 128), i32) for cr in ROWS],
                [pltpu.VMEM((2, n_own, 128), i32) for cr in ROWS],
                [pltpu.SMEM((2, 8, 128), i32) for cr in ROWS],
                [pltpu.SMEM((2, n_own, 128), i32) for cr in ROWS],
                dma((3,)), dma((n_own // GROUP,)), dma((4,)),
                dma((2, 3, LINES, 2)), dma((2, 3, LINES)),
                dma((2, 3)), dma((2, 3)), dma((2, 3)),
                dma((2,)), dma((2, RING)), dma((2,)), dma((2,)),
                dma((2,)), dma((2, 2, n_own // 2 // GROUP)), dma((2, 2, n_own // GROUP)),
            ],
            compiler_params=pltpu.CompilerParams(collective_id=0, has_side_effects=True,
                                                 vmem_limit_bytes=46 * 1024 * 1024),
        )(*[pltpu.with_memory_space_constraint(v, pltpu.HBM) for v in (a, b, pairs, coords, cidx)])
        return out[None]

    return jax.shard_map(per_device, mesh=mesh, in_specs=(dev_spec,) * 5, out_specs=dev_spec, check_vma=False)
```

time: 304 us -> 66.9 us (0.22)
  waiting for transfers between devices: 112 us -> 0 us
  local copies, waits for them, and re-layouts: 91.8 us -> 0.97 us
  matrix products: 68.1 us -> 0 us
  Pallas kernels: 0 us -> 65.8 us
  starting transfers between devices: 22.2 us -> 0 us
  other arithmetic: 6.91 us -> 0 us
    all_to_all x2 -> x0, waiting for transfers between devices: 112 us -> none  [the longest x1 112 us: per_device(): recv_blocks = lax.all_to_all(sent_blocks, 'k', 0, 0, tiled=True)]
    gather x8 -> x0, local copies, waits for them, and re-layouts: 69.7 us -> none  [the longest x4 36.8 us: pair_step(): right_ops = jnp.take(b_blocks, jnp.maximum(pair_rank[:, 1], 0), axis=0)]
    dot_general x5 -> x0, matrix products: 68.1 us -> none  [the longest x4 66.8 us: pair_step(): jnp.einsum('sab,sbc->sac', left_ops, right_ops, preferred_element_type=jn...]
    pallas_call x0 -> x1, Pallas kernels: none -> 65.8 us  [per_device(): pl.pallas_call(kernel, out_shape=jax.ShapeDtypeStruct((n_own, rows, cols)...]
    all_to_all x2 -> x0, starting transfers between devices: 22.2 us -> none  [the longest x1 12 us: per_device(): lax.all_to_all(coord_loc[0].reshape(groups, seg_len, 2), 'k', 0, 0, tiled...]
    all_to_all x2 -> x0, local copies, waits for them, and re-layouts: 8.21 us -> none  [the longest x1 7.3 us: per_device(): recv_blocks = lax.all_to_all(sent_blocks, 'k', 0, 0, tiled=True)]
    reshape x2 -> x0, local copies, waits for them, and re-layouts: 8.18 us -> none  [the longest x1 8.05 us: per_device(): scan_out[0].astype(jnp.bfloat16)]
    convert_element_type x1 -> x0, other arithmetic: 6.65 us -> none  [per_device(): scan_out[0].astype(jnp.bfloat16)]
  transfers between devices with their start and end apart: 2 -> 0, of which waited for: 1 -> 0; matrix products, arithmetic and copies ran while one was open for 52% -> 0% of each run, Pallas kernels for 0% -> 0%
where the time goes in v5:
time: 66.9 us; the launch traced here: 66.7 us
  Pallas kernels  65.8 us (98%)
  local copies, waits for them, and re-layouts  0.97 us (1%)
    pallas_call x1, Pallas kernels, per_device(): pl.pallas_call(kernel, out_shape=jax.ShapeDtypeStruct((n_own, rows, cols)...  65.8 us

profile of v5, /device:TPU:1, one launch (start us, length us, event | category | flops | bytes accessed | tf_op | source)
XLA Modules:
  0.0 66.7 jit_solution(16152221801957219450)
XLA Ops:
  0.0 65.8 %shard_map.55 = f32[16,128,128]{2,1,0:T(8,128)S(1)} custom-call(bf16[4,128,128]{2,1,0:T(8,128)(2,1)} %bitcast.13, bf16[4,128,128]{2,1,0:T(8,128)(2,1)} %bitcast.14, s32[4,2,256]{2,1,0:T(2,128)} %bitcast.15, s32[2,256]{1,0:T(2,128)} %bitcast.16, s32[2,16]{1,0:T(2,128)} %bitcast.17), custom_call_target="tpu_custom_call" | custom-call | tf_op jit(solution)/shard_map/pallas_call | solution.py:470
  65.8 1.0 %copy.7 = f32[1,16,128,128]{3,2,1,0:T(8,128)} copy(f32[1,16,128,128]{3,2,1,0:T(8,128)S(1)} %bitcast.12) | data formatting | bytes 2097152

commit v6 on v5

--- a/solution.py
+++ b/solution.py
@@ -234,7 +234,7 @@
             return tuple(picked)
 
         none = jnp.zeros((8, 128), jnp.int32)
-        picked = lax.fori_loop(0, LINES, pick, (none, none), unroll=8)
+        picked = lax.fori_loop(0, LINES, pick, (none, none), unroll=4)
         for core in (0, 1):
             tblv[p][core] = picked[core]
         sub = lax.broadcasted_iota(jnp.int32, (n_own, 128), 0)
@@ -383,17 +383,17 @@
     side_near(NEXT, XZ, B)
     side_near(OWN, XY, A)
     line_near(XY, A)
+    build_tables(XZ)
     t_sides(XY)
     line_far(XZ, B)
     line_far(XZ, A)
     build_tables(XY)
+    for p in PASSES:
+        for cp in smem_copies(p):
+            cp.start()
     side_near(PREV, XZ, B)
     side_far(OWN, XY, B)
     line_far(XY, B)
-    build_tables(XZ)
-    for p in PASSES:
-        for cp in smem_copies(p):
-            cp.start()
     side_far(OWN, XZ, B)
     line_far(XY, A)
     for p in PASSES:
@@ -403,17 +403,16 @@
     def step_a(n):
         df = order_of(n)
         both(XY, df, 0)
-        both(XZ, df, 0)
         at(n, 0, (side_near, NEXT, XY, B), (side_near, NEXT, XZ, A))
         at(n, 2, (side_near, PREV, XY, B), (side_near, PREV, XZ, A))
         at(n, 3, (side_far, OWN, XY, A), (side_far, OWN, XZ, A))
+        both(XZ, df, 0)
     loop(4, step_a)
 
     def step_b(n):
         df = order_of(n // 2)
         ds = 1 + 2 * (n % 2)
         both(XY, df, ds)
-        both(XZ, df, ds)
         at(n, 0, (side_near, NEXT, XY, A))
         at(n, 1, (side_near, PREV, XY, A), (side_far, NEXT, XZ, B))
         at(n, 3, (side_near, FAR, XY, B))
@@ -421,6 +420,7 @@
         at(n, 5, (side_near, FAR, XZ, B), (side_far, NEXT, XY, B), (side_far, PREV, XY, B), (side_far, NEXT, XY, A), (side_near, FAR, XZ, A))
         at(n, 6, (side_far, PREV, XY, A))
         at(n, 7, (side_far, FAR, XY, B), (side_far, FAR, XY, A))
+        both(XZ, df, ds)
     loop(8, step_b)
 
     def step_c(n):
@@ -430,15 +430,15 @@
     loop(4, step_c)
     far(XY)
     side_far(PREV, XZ, A)
-    near(XY)
-    side_far(FAR, XZ, B)
-    side_far(FAR, XZ, A)
 
     def step_d(n):
+        at(n, 2, (side_far, FAR, XZ, B))
+        at(n, 3, (side_far, FAR, XZ, A))
         both(XZ, order_of(n), 2)
-    loop(4, step_d)
+    loop(RING, step_d)
     far(XZ)
     near(XZ)
+    near(XY)
     combined(XY)
     combined(XZ)
     mine(XY)

time: 66.9 us -> 65.7 us (0.982)
  Pallas kernels: 65.8 us -> 64.6 us
    pallas_call x1, Pallas kernels: 65.8 us -> 64.6 us  [per_device(): pl.pallas_call(kernel, out_shape=jax.ShapeDtypeStruct((n_own, rows, cols)...]
where the time goes in v6:
time: 65.7 us; the launch traced here: 65.6 us
  Pallas kernels  64.6 us (98%)
  local copies, waits for them, and re-layouts  0.97 us (1%)
    pallas_call x1, Pallas kernels, per_device(): pl.pallas_call(kernel, out_shape=jax.ShapeDtypeStruct((n_own, rows, cols)...  64.6 us

profile of v6, /device:TPU:1, one launch (start us, length us, event | category | flops | bytes accessed | tf_op | source)
XLA Modules:
  0.0 65.6 jit_solution(8665430736472712828)
XLA Ops:
  0.0 64.6 %shard_map.55 = f32[16,128,128]{2,1,0:T(8,128)S(1)} custom-call(bf16[4,128,128]{2,1,0:T(8,128)(2,1)} %bitcast.13, bf16[4,128,128]{2,1,0:T(8,128)(2,1)} %bitcast.14, s32[4,2,256]{2,1,0:T(2,128)} %bitcast.15, s32[2,256]{1,0:T(2,128)} %bitcast.16, s32[2,16]{1,0:T(2,128)} %bitcast.17), custom_call_target="tpu_custom_call" | custom-call | tf_op jit(solution)/shard_map/pallas_call | solution.py:470
  64.6 1.0 %copy.7 = f32[1,16,128,128]{3,2,1,0:T(8,128)} copy(f32[1,16,128,128]{3,2,1,0:T(8,128)S(1)} %bitcast.12) | data formatting | bytes 2097152

commit v7 on v6

--- a/solution.py
+++ b/solution.py
@@ -278,12 +278,14 @@
                 total = total + prod[tbl_s[p][core, u, at_lane], span]
             parts[p][src * SLOTS + j] = total.astype(jnp.bfloat16).astype(jnp.float32)
 
-    def both(p, df, ds):
-        slot = slot_of(p, 1 - c, df, ds)
-        for k in (0, 1):
-            bytes_wait(whole(p, k, 1 - c, slot), sib_sem.at[p, k, slot])
-        compute(p, c, slot_of(p, c, df, ds), prods[0])
-        compute(p, 1 - c, slot, prods[1])
+    def products(todo, ds):
+        for p, df in todo:
+            slot = slot_of(p, 1 - c, df, ds)
+            for k in (B, A):
+                bytes_wait(whole(p, k, 1 - c, slot), sib_sem.at[p, k, slot])
+        for i, (p, df) in enumerate(todo):
+            compute(p, c, slot_of(p, c, df, ds), prods[2 * i])
+            compute(p, 1 - c, slot_of(p, 1 - c, df, ds), prods[2 * i + 1])
 
     def loop(n, body):
         def run(j, carry):
@@ -402,17 +404,16 @@
 
     def step_a(n):
         df = order_of(n)
-        both(XY, df, 0)
+        products([(p, df) for p in PASSES], 0)
         at(n, 0, (side_near, NEXT, XY, B), (side_near, NEXT, XZ, A))
         at(n, 2, (side_near, PREV, XY, B), (side_near, PREV, XZ, A))
         at(n, 3, (side_far, OWN, XY, A), (side_far, OWN, XZ, A))
-        both(XZ, df, 0)
     loop(4, step_a)
 
     def step_b(n):
         df = order_of(n // 2)
         ds = 1 + 2 * (n % 2)
-        both(XY, df, ds)
+        products([(p, df) for p in PASSES], ds)
         at(n, 0, (side_near, NEXT, XY, A))
         at(n, 1, (side_near, PREV, XY, A), (side_far, NEXT, XZ, B))
         at(n, 3, (side_near, FAR, XY, B))
@@ -420,22 +421,20 @@
         at(n, 5, (side_near, FAR, XZ, B), (side_far, NEXT, XY, B), (side_far, PREV, XY, B), (side_far, NEXT, XY, A), (side_near, FAR, XZ, A))
         at(n, 6, (side_far, PREV, XY, A))
         at(n, 7, (side_far, FAR, XY, B), (side_far, FAR, XY, A))
-        both(XZ, df, ds)
     loop(8, step_b)
 
     def step_c(n):
-        both(XY, order_of(n), 2)
         at(n, 0, (side_far, PREV, XZ, B))
-        at(n, 2, (side_far, NEXT, XZ, A))
-    loop(4, step_c)
+        products([(XY, order_of(2 * n + i)) for i in range(2)], FAR)
+        at(n, 0, (side_far, NEXT, XZ, A))
+    loop(2, step_c)
     far(XY)
     side_far(PREV, XZ, A)
 
     def step_d(n):
-        at(n, 2, (side_far, FAR, XZ, B))
-        at(n, 3, (side_far, FAR, XZ, A))
-        both(XZ, order_of(n), 2)
-    loop(RING, step_d)
+        at(n, 1, (side_far, FAR, XZ, B), (side_far, FAR, XZ, A))
+        products([(XZ, order_of(2 * n + i)) for i in range(2)], FAR)
+    loop(2, step_d)
     far(XZ)
     near(XZ)
     near(XY)
@@ -478,7 +477,7 @@
                 [pltpu.VMEM((2, LINES, 4, depth, cols), bf16) for cr in ROWS],
                 [pltpu.VMEM((2, LINES, 4, cr, depth), bf16) for cr in ROWS],
                 [pltpu.VMEM((2, LINES, 2, 8, 128), i32) for cr in ROWS],
-                [pltpu.VMEM((NOPAIR + 1, max(ROWS), cols), f32) for _ in range(2)],
+                [pltpu.VMEM((NOPAIR + 1, max(ROWS), cols), f32) for _ in range(4)],
                 [pltpu.VMEM((NOSLOT + 1, cr, cols), f32) for cr in ROWS],
                 [pltpu.VMEM((RING, n_own, cr, cols), f32) for cr in ROWS],
                 [pltpu.VMEM((2, n_own // 2, cr, cols), f32) for cr in ROWS],
@@ -495,7 +494,7 @@
                 dma((2,)), dma((2, 2, n_own // 2 // GROUP)), dma((2, 2, n_own // GROUP)),
             ],
             compiler_params=pltpu.CompilerParams(collective_id=0, has_side_effects=True,
-                                                 vmem_limit_bytes=46 * 1024 * 1024),
+                                                 vmem_limit_bytes=48 * 1024 * 1024),
         )(*[pltpu.with_memory_space_constraint(v, pltpu.HBM) for v in (a, b, pairs, coords, cidx)])
         return out[None]
 

time: 65.7 us -> 63.9 us (0.973)
  Pallas kernels: 64.6 us -> 62.8 us
    pallas_call x1, Pallas kernels: 64.6 us -> 62.8 us  [per_device(): pl.pallas_call(kernel, out_shape=jax.ShapeDtypeStruct((n_own, rows, cols)...]
where the time goes in v7:
time: 63.9 us; the launch traced here: 63.8 us
  Pallas kernels  62.8 us (98%)
  local copies, waits for them, and re-layouts  0.97 us (2%)
    pallas_call x1, Pallas kernels, per_device(): pl.pallas_call(kernel, out_shape=jax.ShapeDtypeStruct((n_own, rows, cols)...  62.8 us

profile of v7, /device:TPU:1, one launch (start us, length us, event | category | flops | bytes accessed | tf_op | source)
XLA Modules:
  0.0 63.8 jit_solution(16021013748299020196)
XLA Ops:
  0.0 62.8 %shard_map.55 = f32[16,128,128]{2,1,0:T(8,128)S(1)} custom-call(bf16[4,128,128]{2,1,0:T(8,128)(2,1)} %bitcast.13, bf16[4,128,128]{2,1,0:T(8,128)(2,1)} %bitcast.14, s32[4,2,256]{2,1,0:T(2,128)} %bitcast.15, s32[2,256]{1,0:T(2,128)} %bitcast.16, s32[2,16]{1,0:T(2,128)} %bitcast.17), custom_call_target="tpu_custom_call" | custom-call | tf_op jit(solution)/shard_map/pallas_call | solution.py:469
  62.9 1.0 %copy.7 = f32[1,16,128,128]{3,2,1,0:T(8,128)} copy(f32[1,16,128,128]{3,2,1,0:T(8,128)S(1)} %bitcast.12) | data formatting | bytes 2097152
